TPU v7x, 32 devices: a whole 2x2x4 slice. The times are simulated.
32 devices in a mesh: data: 32 (over z, y, x, core).
Axes of the slice: x: 2, y: 2, z: 4, core: 2. Of those that a mesh axis runs over, the one named last changes fastest.
Arguments:
- x_now: bfloat16 [64, 784, 128], P('data')
- labels_now: int32 [64], P('data')
- x_next: bfloat16 [64, 784, 128], P('data')
- up_one: float32 [4, 128, 512], replicated
- down_one: float32 [4, 512, 128], replicated
- merge_proj: float32 [512, 512], replicated
- up_two: float32 [3, 512, 2048], replicated
- down_two: float32 [3, 2048, 512], replicated
- head_proj: float32 [512, 1000], replicated
- vel_up_one: float32 [4, 128, 512], replicated
- vel_down_one: float32 [4, 512, 128], replicated
- vel_merge_proj: float32 [512, 512], replicated
- vel_up_two: float32 [3, 512, 2048], replicated
- vel_down_two: float32 [3, 2048, 512], replicated
- vel_head_proj: float32 [512, 1000], replicated
Outputs:
- output 1: float32 [64, 1000], P('data')
- output 2: float32 [4, 128, 512], replicated
- output 3: float32 [4, 512, 128], replicated
- output 4: float32 [512, 512], replicated
- output 5: float32 [3, 512, 2048], replicated
- output 6: float32 [3, 2048, 512], replicated
- output 7: float32 [512, 1000], replicated
- output 8: float32 [4, 128, 512], replicated
- output 9: float32 [4, 512, 128], replicated
- output 10: float32 [512, 512], replicated
- output 11: float32 [3, 512, 2048], replicated
- output 12: float32 [3, 2048, 512], replicated
- output 13: float32 [512, 1000], replicated
All inputs are finite; a program needn't handle non-finite values.
Results may differ from a plain program's by a relative error of at most 0.0131016.
Values are sent between devices in bfloat16 or wider.
A program may use at most 1 GiB of HBM per device.

v0:
```python
import jax
import jax.numpy as jnp
from jax import lax
from jax.sharding import PartitionSpec as P

MOMENTUM = 0.9
TRUST = 0.1
LN_EPS = 1e-6


def layer_norm(values):
    row_mean = jnp.mean(values, axis=-1, keepdims=True)
    centered = values - row_mean
    variance = jnp.mean(centered * centered, axis=-1, keepdims=True)
    return centered * lax.rsqrt(variance + LN_EPS)


def gelu_tanh(values):
    return jax.nn.gelu(values, approximate=True)


def contract_rows(lhs_mat, rhs_mat):
    return lax.dot_general(lhs_mat, rhs_mat, (((0,), (0,)), ((), ())), preferred_element_type=jnp.float32)


def contract_cols(lhs_mat, rhs_mat):
    return lax.dot_general(lhs_mat, rhs_mat, (((1,), (1,)), ((), ())), preferred_element_type=jnp.float32)


def to_bf16_layers(stacked):
    return [stacked[layer_num].astype(jnp.bfloat16) for layer_num in range(stacked.shape[0])]


def cast_weights(params):
    up_one, down_one, merge_proj, up_two, down_two, head_proj = params
    return (to_bf16_layers(up_one), to_bf16_layers(down_one), merge_proj.astype(jnp.bfloat16), to_bf16_layers(up_two), to_bf16_layers(down_two), head_proj.astype(jnp.bfloat16))


def block_forward(residual, w_up, w_down):
    normed, norm_back = jax.vjp(layer_norm, residual.astype(jnp.float32))
    normed_b = normed.astype(jnp.bfloat16)
    pre_act = jnp.dot(normed_b, w_up, preferred_element_type=jnp.float32)
    activated, gelu_back = jax.vjp(gelu_tanh, pre_act)
    activated_b = activated.astype(jnp.bfloat16)
    block_out = jnp.dot(activated_b, w_down, preferred_element_type=jnp.float32)
    new_residual = (residual.astype(jnp.float32) + block_out).astype(jnp.bfloat16)
    return new_residual, (normed_b, activated_b, norm_back, gelu_back)


def block_backward(grad_out, saved, w_up, w_down):
    normed_b, activated_b, norm_back, gelu_back = saved
    grad_down = contract_rows(activated_b, grad_out)
    grad_act = contract_cols(grad_out, w_down)
    grad_pre = gelu_back(grad_act)[0].astype(jnp.bfloat16)
    grad_up = contract_rows(normed_b, grad_pre)
    grad_normed = contract_cols(grad_pre, w_up)
    grad_in = norm_back(grad_normed)[0] + grad_out.astype(jnp.float32)
    return grad_in.astype(jnp.bfloat16), grad_up, grad_down


def model_forward(images, weights):
    ups_one, downs_one, merge_w, ups_two, downs_two, head_w = weights
    img_count, tokens, width = images.shape
    residual = images.reshape(img_count * tokens, width)
    saved_one = []
    for w_up, w_down in zip(ups_one, downs_one):
        residual, saved = block_forward(residual, w_up, w_down)
        saved_one.append(saved)
    merged = residual.reshape(img_count * tokens // 4, 4 * width)
    residual = jnp.dot(merged, merge_w, preferred_element_type=jnp.float32).astype(jnp.bfloat16)
    saved_two = []
    for w_up, w_down in zip(ups_two, downs_two):
        residual, saved = block_forward(residual, w_up, w_down)
        saved_two.append(saved)
    pooled = jnp.mean(residual.reshape(img_count, tokens // 4, -1), axis=1, dtype=jnp.float32)
    head_in, head_back = jax.vjp(layer_norm, pooled)
    head_in_b = head_in.astype(jnp.bfloat16)
    logits = jnp.dot(head_in_b, head_w, preferred_element_type=jnp.float32)
    return logits, (saved_one, merged, saved_two, head_in_b, head_back)


def loss_grad(logits, labels, global_batch):
    soft_probs = jax.nn.softmax(logits, axis=-1)
    class_ids = jnp.arange(logits.shape[1], dtype=jnp.int32)
    onehot = (labels[:, None] == class_ids[None, :]).astype(jnp.float32)
    return ((soft_probs - onehot) / global_batch).astype(jnp.bfloat16)


def head_input_grad(grad_logits, head_w, head_back, merged_tokens):
    grad_pooled = head_back(contract_cols(grad_logits, head_w))[0] / merged_tokens
    img_count, width_two = grad_pooled.shape
    spread = jnp.broadcast_to(grad_pooled.astype(jnp.bfloat16)[:, None, :], (img_count, merged_tokens, width_two))
    return spread.reshape(img_count * merged_tokens, width_two)


def lars_step(weight, velocity, grad_sum):
    grad_f = grad_sum.astype(jnp.float32)
    red_axes = (weight.ndim - 2, weight.ndim - 1)
    w_norm = jnp.sqrt(jnp.sum(weight * weight, axis=red_axes, keepdims=True))
    g_norm = jnp.sqrt(jnp.sum(grad_f * grad_f, axis=red_axes, keepdims=True))
    new_vel = MOMENTUM * velocity + TRUST * (w_norm / g_norm) * grad_f
    return weight - new_vel, new_vel


def finish_step(params, velocities, grad_sums, x_next):
    updated = [lars_step(weight, velocity, grad_sum) for weight, velocity, grad_sum in zip(params, velocities, grad_sums)]
    new_params = tuple(pair_new[0] for pair_new in updated)
    new_vels = tuple(pair_new[1] for pair_new in updated)
    logits_next = model_forward(x_next, cast_weights(new_params))[0]
    return (logits_next,) + new_params + new_vels


def solution(mesh):
    data_devs = mesh.shape['data']

    def local_step(x_now, labels_now, x_next, up_one, down_one, merge_proj, up_two, down_two, head_proj, vel_up_one, vel_down_one, vel_merge_proj, vel_up_two, vel_down_two, vel_head_proj):
        params = (up_one, down_one, merge_proj, up_two, down_two, head_proj)
        velocities = (vel_up_one, vel_down_one, vel_merge_proj, vel_up_two, vel_down_two, vel_head_proj)
        weights = cast_weights(params)
        ups_one, downs_one, merge_w, ups_two, downs_two, head_w = weights
        img_count, tokens, width = x_now.shape
        depth_one = len(ups_one)
        depth_two = len(ups_two)
        logits, saved = model_forward(x_now, weights)
        saved_one, merged, saved_two, head_in_b, head_back = saved
        grad_logits = loss_grad(logits, labels_now, img_count * data_devs)
        sum_head = lax.psum(contract_rows(head_in_b, grad_logits).astype(jnp.bfloat16), 'data')
        grad_resid = head_input_grad(grad_logits, head_w, head_back, tokens // 4)
        sums_up_two = [None] * depth_two
        sums_down_two = [None] * depth_two
        for layer_num in reversed(range(depth_two)):
            grad_resid, grad_up, grad_down = block_backward(grad_resid, saved_two[layer_num], ups_two[layer_num], downs_two[layer_num])
            sums_down_two[layer_num] = lax.psum(grad_down.astype(jnp.bfloat16), 'data')
            sums_up_two[layer_num] = lax.psum(grad_up.astype(jnp.bfloat16), 'data')
        sum_merge = lax.psum(contract_rows(merged, grad_resid).astype(jnp.bfloat16), 'data')
        grad_resid = contract_cols(grad_resid, merge_w).astype(jnp.bfloat16).reshape(img_count * tokens, width)
        sums_up_one = [None] * depth_one
        sums_down_one = [None] * depth_one
        for layer_num in reversed(range(depth_one)):
            grad_resid, grad_up, grad_down = block_backward(grad_resid, saved_one[layer_num], ups_one[layer_num], downs_one[layer_num])
            sums_down_one[layer_num] = lax.psum(grad_down.astype(jnp.bfloat16), 'data')
            sums_up_one[layer_num] = lax.psum(grad_up.astype(jnp.bfloat16), 'data')
        grad_sums = (jnp.stack(sums_up_one), jnp.stack(sums_down_one), sum_merge, jnp.stack(sums_up_two), jnp.stack(sums_down_two), sum_head)
        return finish_step(params, velocities, grad_sums, x_next)

    replicated = P()
    batch_split = P('data')
    in_specs = (batch_split, batch_split, batch_split) + (replicated,) * 12
    out_specs = (batch_split,) + (replicated,) * 12
    return jax.shard_map(local_step, mesh=mesh, in_specs=in_specs, out_specs=out_specs, check_vma=False)
```

profile of v0, /device:TPU:0, one launch (start us, length us, event | category | flops | bytes accessed | tf_op | source)
XLA Modules:
  0.0 810.6 jit_solution(17480342943118579962)
XLA Ops:
  7.2 2.3 multiply_reduce_fusion.5
  23.4 3.2 multiply_convert_fusion.3
  32.2 13.1 %multiply_reduce_fusion.1 = (f32[3]{0:T(128)S(1)}, bf16[3,512,2048]{2,1,0:T(8,128)(2,1)}) fusion(f32[3,512,2048]{2,1,0:T(8,128)} %param.21), kind=kLoop, calls=%fused_computation.9 | loop fusion | flops 9437181 | bytes 18874380 | tf_op jit(solution)/shard_map/reduce_sum | solution.py:99
  45.3 13.8 %multiply_reduce_fusion = (f32[3]{0:T(128)}, bf16[3,2048,512]{2,1,0:T(8,128)(2,1)}) fusion(f32[3,2048,512]{2,1,0:T(8,128)} %param.22), kind=kLoop, calls=%fused_computation.8 | loop fusion | flops 9437181 | bytes 18874380 | tf_op jit(solution)/shard_map/reduce_sum | solution.py:99
  59.1 2.8 fusion.139
  61.9 4.1 fusion.301
  67.5 4.1 fusion.302
  74.6 4.6 fusion.155
  79.2 2.3 reshape.479
  85.2 1.8 reshape.474
  87.0 6.0 fusion.52
  93.1 2.9 multiply_reduce_fusion.17
  97.9 4.4 fusion.45
  103.5 2.7 fusion.110
  106.3 2.8 fusion.111
  110.9 4.6 fusion.38
  115.5 2.9 fusion.112
  118.4 2.9 fusion.113
  121.3 2.9 fusion.114
  124.1 2.8 fusion.109
  131.6 2.0 reshape.475
  133.6 4.6 fusion.31
  140.4 2.5 fusion.24
  144.9 2.5 fusion.17
  151.4 1.7 fusion.171
  153.1 2.0 fusion.173
  155.2 2.0 fusion.174
  162.3 2.0 fusion.172
  164.4 5.1 fusion.176
  176.2 517.2 %all-reduce.3.cloned.1.call-done = (bf16[512,1000]{0,1:T(8,128)(2,1)}, bf16[1,512,128]{2,1,0:T(8,128)(2,1)}, bf16[1,512,128]{2,1,0:T(8,128)(2,1)}, bf16[1,512,12...) async-done(((bf16[512,1000]{0,1:T(8,128)(2,1)}, ...) | async-done | bytes 15179792 | tf_op jit(solution)/shard_map/psum | solution.py:127
  693.4 1.9 fusion.181
  697.5 3.7 fusion.284
  701.5 1.8 fusion.286
  703.4 3.3 fusion.304
  708.4 4.0 fusion.305
  714.1 3.9 fusion.306
  717.9 2.1 multiply_reduce_fusion.9
  720.0 3.8 fusion.128
  725.1 2.9 fusion.282
  729.6 2.1 fusion
  731.8 23.6 %fusion.278 = (bf16[3,512,2048]{2,1,0:T(8,128)(2,1)}, f32[3,512,2048]{2,1,0:T(8,128)}, f32[3,512,2048]{2,1,0:T(8,128)}) fusion(f32[3,512,2048]{2,1,0:T(8,128)} %param.21, bf16[1,512,2048]{2,1,0:T(8,128)(2,1)S(1)} %copy-done.17, bf16[1,512,2048]{2,1,0:T(8,128)(2,1)S(1)} %copy-done.18, bf16[1,512,2048]{2,1,0:T(8,128)(2,1)} %get-tuple-element.28, ...), kind=kLoop, calls=%fused_computation.478 | loop fusion | flops 25165824 | bytes 62914572 | tf_op jit(solution)/shard_map/convert.9
  755.5 1.9 fusion.2
  757.4 17.8 %fusion.280 = (bf16[3,2048,512]{2,1,0:T(8,128)(2,1)}, f32[3,2048,512]{2,1,0:T(8,128)}, f32[3,2048,512]{2,1,0:T(8,128)}) fusion(f32[3,2048,512]{2,1,0:T(8,128)S(1)} %bitcast.270, bf16[1,2048,512]{2,1,0:T(8,128)(2,1)} %get-tuple-element.23, bf16[1,2048,512]{2,1,0:T(8,128)(2,1)} %get-tuple-element.24, bf16[1,2048,512]{2,1,0:T(8,128)(2,1)} %get-tuple-element.25, ...), kind=kLoop, calls=%fused_computation.479 | loop fusion | flops 25165824 | bytes 62914572 | tf_op jit(solution)/shard_map/convert.8
  775.2 5.0 fusion.308
  780.5 5.4 fusion.309
  787.3 5.9 fusion.157
  793.2 2.1 reshape.480
  798.6 3.6 fusion.288
  (259 shorter events, 69.1 us)
Async XLA Ops:
  7.2 6.9 copy-start.28
  7.2 686.2 %all-reduce.3.cloned.1.call-start = ((), (), s32[]{:S(2)}) async-start(), calls=%async_computation | async-start | bytes 30359552 | tf_op jit(solution)/shard_map/psum | solution.py:127
  9.5 13.9 %copy-start.33 = (bf16[4,128,512]{2,1,0:T(8,128)(2,1)}, bf16[4,128,512]{2,1,0:T(8,128)(2,1)S(1)}, u32[]{:S(2)}) copy-start(bf16[4,128,512]{2,1,0:T(8,128)(2,1)S(1)} %get-tuple-element.66) | copy-start | bytes 1572868
  11.0 4.4 copy-start.21
  14.8 6.4 copy-start.52
  17.1 2.5 copy-start.1
  20.0 2.5 copy-start.3
  26.7 3.7 copy-start.5
  31.9 30.0 %copy-start.8 = (f32[392,512]{1,0:T(8,128)}, f32[392,512]{1,0:T(8,128)S(1)}, u32[]{:S(2)}) copy-start(f32[392,512]{1,0:T(8,128)S(1)} %get-tuple-element.78) | copy-start | bytes 2408452
  59.1 7.2 slice-start.3
  61.9 4.1 copy-start.22
  61.9 4.4 slice-start.4
  67.4 4.1 copy-start.24
  79.2 3.8 copy-start
  79.2 4.5 copy-start.54
  87.0 6.1 copy-start.13
  93.1 3.3 copy-start.46
  96.3 6.0 slice-start.5
  97.9 4.5 slice-start.6
  97.9 4.5 copy-start.11
  118.4 2.9 copy-start.27
  121.3 2.9 copy-start.9
  128.0 2.3 copy-start.6
  133.6 4.6 copy-start.34
  138.3 2.1 copy-start.53
  140.4 2.5 copy-start.4
  144.9 2.5 copy-start.2
  158.5 3.8 copy-start.36
  170.7 3.4 copy-start.32
  170.7 526.8 %copy-start.57 = (f32[4]{0:T(128)S(1)}, f32[4]{0:T(128)}, u32[]{:S(2)}) copy-start(f32[4]{0:T(128)} %get-tuple-element.65) | copy-start | bytes 52
  695.3 6.2 copy-start.56
  696.0 5.3 copy-start.48
  696.0 5.3 copy-start.49
  696.0 5.3 copy-start.50
  696.0 5.3 copy-start.51
  696.0 5.5 copy-start.29
  696.0 5.5 copy-start.47
  725.1 4.5 copy-start.17
  725.1 4.5 copy-start.18
  725.1 4.5 copy-start.19
  728.0 3.8 copy-start.30
  731.8 25.6 %slice-start = ((s8[12582912]{0:T(1024)(128)(4,1)}), s8[4194304]{0:T(1024)(128)(4,1)S(1)}, s32[]{:S(2)}) async-start(s8[12582912]{0:T(1024)(128)(4,1)} %bitcast.269), calls=%async_computation.1 | async-start | bytes 8388608
  731.8 23.6 %copy-start.14 = (bf16[1,2048,512]{2,1,0:T(8,128)(2,1)S(1)}, bf16[1,2048,512]{2,1,0:T(8,128)(2,1)}, u32[]{:S(2)}) copy-start(bf16[1,2048,512]{2,1,0:T(8,128)(2,1)} %get-tuple-element.23) | copy-start | bytes 6291460
  731.8 23.6 %copy-start.15 = (bf16[1,2048,512]{2,1,0:T(8,128)(2,1)S(1)}, bf16[1,2048,512]{2,1,0:T(8,128)(2,1)}, u32[]{:S(2)}) copy-start(bf16[1,2048,512]{2,1,0:T(8,128)(2,1)} %get-tuple-element.24) | copy-start | bytes 6291460
  731.8 23.6 %copy-start.16 = (bf16[1,2048,512]{2,1,0:T(8,128)(2,1)S(1)}, bf16[1,2048,512]{2,1,0:T(8,128)(2,1)}, u32[]{:S(2)}) copy-start(bf16[1,2048,512]{2,1,0:T(8,128)(2,1)} %get-tuple-element.25) | copy-start | bytes 6291460
  731.8 25.6 %slice-start.1 = ((s8[12582912]{0:T(1024)(128)(4,1)}), s8[4194304]{0:T(1024)(128)(4,1)S(1)}, s32[]{:S(2)}) async-start(s8[12582912]{0:T(1024)(128)(4,1)} %bitcast.269), calls=%async_computation.2 | async-start | bytes 8388608
  731.8 25.6 %slice-start.2 = ((s8[12582912]{0:T(1024)(128)(4,1)}), s8[4194304]{0:T(1024)(128)(4,1)S(1)}, s32[]{:S(2)}) async-start(s8[12582912]{0:T(1024)(128)(4,1)} %bitcast.269), calls=%async_computation.3 | async-start | bytes 8388608
  787.2 9.5 %copy-start.31 = (bf16[512,1000]{0,1:T(8,128)(2,1)S(1)}, bf16[512,1000]{0,1:T(8,128)(2,1)}, u32[]{:S(2)}) copy-start(bf16[512,1000]{0,1:T(8,128)(2,1)} %get-tuple-element.13) | copy-start | bytes 3072004
  (18 other events, 28.7 us)
Sparse Core Ops, SparseCore 0:
  169.7 523.6 all-reduce.2
where the time goes:
time: 818 us; the launch traced here: 811 us
  waiting for transfers between devices  517 us (63%)
  matrix products  134 us (16%)
  other arithmetic  120 us (15%)
  local copies, waits for them, and re-layouts  21 us (3%)
  between operations  18.1 us (2%)
    psum x1, waiting for transfers between devices, local_step(): lax.psum(contract_rows(head_in_b, grad_logits).astype(jnp.bfloat16), 'data')  517 us
    dot_general x14, matrix products, block_forward(): block_out = jnp.dot(activated_b, w_down, preferred_element_type=jnp.float32)  49.5 us
    another operation x4, other arithmetic  46.9 us
    dot_general x16, matrix products, contract_rows(): lax.dot_general(lhs_mat, rhs_mat, (((0,), (0,)), ((), ())), preferred_ele...  37.3 us
    dot_general x14, matrix products, contract_cols(): lax.dot_general(lhs_mat, rhs_mat, (((1,), (1,)), ((), ())), preferred_ele...  33.5 us
    reduce_sum x6, other arithmetic, lars_step(): w_norm = jnp.sqrt(jnp.sum(weight * weight, axis=red_axes, keepdims=True))  31.9 us
  transfers between devices with their start and end apart: 1, of which 1 were waited for; matrix products, arithmetic and copies ran while one was open for 0% of the time, Pallas kernels for 0%

commit v1 on v0

--- a/solution.py
+++ b/solution.py
@@ -1,6 +1,10 @@
+import functools
+
 import jax
 import jax.numpy as jnp
 from jax import lax
+from jax.experimental import pallas as pl
+from jax.experimental.pallas import tpu as pltpu
 from jax.sharding import PartitionSpec as P
 
 MOMENTUM = 0.9
@@ -110,6 +114,267 @@
     return (logits_next,) + new_params + new_vels
 
 
+MESH = pl.DeviceIdType.MESH
+ROWS = 512
+LAG = 2
+STAGES = 12
+
+
+def all_reduce_body(chunks, grad_buf, full_buf, recv_core, recv_one, recv_z, recv_mid, recv_two, send_sem, recv_sem, before, after):
+    me = lax.axis_index('data')
+    core = me % 2
+    x_pos = (me // 2) % 2
+    y_pos = (me // 4) % 2
+    z_pos = me // 8
+    one = x_pos * (1 - core) + y_pos * core
+    two = y_pos * (1 - core) + x_pos * core
+    one_step = 2 * (1 - core) + 4 * core
+    two_step = 4 * (1 - core) + 2 * core
+    dev_core = me + 1 - 2 * core
+    dev_one = me + one_step * (1 - 2 * one)
+    dev_two = me + two_step * (1 - 2 * two)
+    upper = z_pos // 2
+    is_end = (z_pos % 3) == 0
+    is_mid = (z_pos % 3) != 0
+    dev_inner = me + 8 * (1 - 2 * upper)
+    dev_outer = me - 8 * (1 - 2 * upper)
+    half = core * 256
+    quarter = half + one * 128
+    near = quarter + upper * 64
+    far = quarter + (1 - upper) * 64
+    mine = near + two * 32
+
+    def rows(chunk, start, size):
+        return grad_buf.at[chunk, pl.ds(pl.multiple_of(start, 32), size)]
+
+    def full(chunk, start, size):
+        return full_buf.at[chunk, pl.ds(pl.multiple_of(start, 32), size)]
+
+    def remote(src, dst, which, chunk, dev):
+        return pltpu.make_async_remote_copy(src_ref=src, dst_ref=dst, send_sem=send_sem.at[which, chunk], recv_sem=recv_sem.at[which, chunk], device_id=(dev,), device_id_type=MESH)
+
+    def add_in(chunk, start, size, recv):
+        def step(num, carry):
+            spot = pl.ds(pl.multiple_of(start + num * 32, 32), 32)
+            grad_buf[chunk, spot, :] = grad_buf[chunk, spot, :] + recv[chunk, pl.ds(pl.multiple_of(num * 32, 32), 32), :]
+            return carry
+        lax.fori_loop(0, size // 32, step, 0)
+
+    def c_core(k):
+        return remote(rows(k, 256 - half, 256), recv_core.at[k], 0, k, dev_core)
+
+    def c_one(k):
+        return remote(rows(k, half + (1 - one) * 128, 128), recv_one.at[k], 1, k, dev_one)
+
+    def c_in(k):
+        return remote(rows(k, far, 64), recv_z.at[k], 2, k, dev_inner)
+
+    def c_mid(k):
+        return remote(rows(k, far, 64), recv_mid.at[k], 3, k, dev_inner)
+
+    def c_out(k):
+        return remote(rows(k, near, 64), recv_z.at[k], 2, k, dev_outer)
+
+    def c_two(k):
+        return remote(rows(k, near + (1 - two) * 32, 32), recv_two.at[k], 4, k, dev_two)
+
+    def g_two(k):
+        return remote(full(k, mine, 32), full(k, mine, 32), 5, k, dev_two)
+
+    def g_in(k):
+        return remote(full(k, near, 64), full(k, near, 64), 6, k, dev_inner)
+
+    def g_mid(k):
+        return remote(full(k, near, 64), full(k, near, 64), 7, k, dev_inner)
+
+    def g_out(k):
+        return remote(full(k, far, 64), full(k, far, 64), 6, k, dev_outer)
+
+    def g_one(k):
+        return remote(full(k, quarter, 128), full(k, quarter, 128), 8, k, dev_one)
+
+    def g_core(k):
+        return remote(full(k, half, 256), full(k, half, 256), 9, k, dev_core)
+
+    def stage_0(k):
+        before(k)
+        c_core(k).start()
+
+    def stage_1(k):
+        c_core(k).wait()
+        add_in(k, half, 256, recv_core)
+        c_one(k).start()
+
+    def stage_2(k):
+        c_one(k).wait()
+        add_in(k, quarter, 128, recv_one)
+        @pl.when(is_end)
+        def _():
+            c_in(k).start()
+
+    def stage_3(k):
+        @pl.when(is_end)
+        def _():
+            c_in(k).wait_send()
+        @pl.when(is_mid)
+        def _():
+            c_out(k).wait_recv()
+            add_in(k, far, 64, recv_z)
+            c_mid(k).start()
+
+    def stage_4(k):
+        @pl.when(is_mid)
+        def _():
+            c_mid(k).wait()
+            add_in(k, near, 64, recv_mid)
+            c_out(k).start()
+
+    def stage_5(k):
+        @pl.when(is_mid)
+        def _():
+            c_out(k).wait_send()
+        @pl.when(is_end)
+        def _():
+            c_in(k).wait_recv()
+            add_in(k, near, 64, recv_z)
+            c_two(k).start()
+
+    def stage_6(k):
+        @pl.when(is_end)
+        def _():
+            c_two(k).wait()
+            spot = pl.ds(pl.multiple_of(mine, 32), 32)
+            full_buf[k, spot, :] = grad_buf[k, spot, :] + recv_two[k]
+            g_two(k).start()
+
+    def stage_7(k):
+        @pl.when(is_end)
+        def _():
+            g_two(k).wait()
+            g_in(k).start()
+
+    def stage_8(k):
+        @pl.when(is_end)
+        def _():
+            g_in(k).wait_send()
+        @pl.when(is_mid)
+        def _():
+            g_out(k).wait_recv()
+            g_mid(k).start()
+
+    def stage_9(k):
+        @pl.when(is_mid)
+        def _():
+            g_mid(k).wait()
+            g_out(k).start()
+
+    def stage_10(k):
+        @pl.when(is_mid)
+        def _():
+            g_out(k).wait_send()
+        @pl.when(is_end)
+        def _():
+            g_in(k).wait_recv()
+        g_one(k).start()
+
+    def stage_11(k):
+        g_one(k).wait()
+        g_core(k).start()
+
+    def stage_12(k):
+        g_core(k).wait()
+        after(k)
+
+    stages = (stage_0, stage_1, stage_2, stage_3, stage_4, stage_5, stage_6, stage_7, stage_8, stage_9, stage_10, stage_11, stage_12)
+
+    def tick(t, carry):
+        for num, stage in enumerate(stages):
+            k = t - num * LAG
+            pl.when((k >= 0) & (k < chunks))(functools.partial(stage, k))
+        return carry
+
+    lax.fori_loop(0, chunks + STAGES * LAG, tick, 0)
+
+
+def scratch(chunks, cols):
+    return [
+        pltpu.VMEM((chunks, 512, cols), jnp.bfloat16),
+        pltpu.VMEM((chunks, 512, cols), jnp.bfloat16),
+        pltpu.VMEM((chunks, 256, cols), jnp.bfloat16),
+        pltpu.VMEM((chunks, 128, cols), jnp.bfloat16),
+        pltpu.VMEM((chunks, 64, cols), jnp.bfloat16),
+        pltpu.VMEM((chunks, 64, cols), jnp.bfloat16),
+        pltpu.VMEM((chunks, 32, cols), jnp.bfloat16),
+        pltpu.SemaphoreType.DMA((10, chunks)),
+        pltpu.SemaphoreType.DMA((10, chunks)),
+    ]
+
+
+def windows(up_one, down_one, merge, up_two, down_two, head):
+    table = []
+    for layer in reversed(range(3)):
+        for part in range(4):
+            table.append([(down_two, (layer, pl.ds(part * 512, 512)), (pl.ds(0, 512),))])
+        for part in range(4):
+            table.append([(up_two, (layer, pl.ds(0, 512), pl.ds(part * 512, 512)), (pl.ds(0, 512),))])
+    for part in range(2):
+        table.append([(head, (pl.ds(0, 512), pl.ds(part * 512, 512)), (pl.ds(0, 512),))])
+    table.append([(merge, (pl.ds(0, 512),), (pl.ds(0, 512),))])
+    table.append([(down_one, (layer,), (pl.ds(0, 512), pl.ds(layer * 128, 128))) for layer in range(4)])
+    table.append([(up_one, (layer,), (pl.ds(layer * 128, 128),)) for layer in range(4)])
+    return table
+
+
+CHUNKS = 29
+
+
+def reduce_kernel(*refs):
+    ups_one, downs_one, merge, ups_two, downs_two, head = refs[0:4], refs[4:8], refs[8], refs[9:12], refs[12:15], refs[15]
+    outs = refs[16:22]
+    load_sem, out_sem = refs[22:24]
+    bufs = refs[24:]
+    grad_buf, full_buf = bufs[0:2]
+    loads = windows(ups_one, downs_one, merge, ups_two, downs_two, head)
+    stores = windows(*outs)
+
+    def place(array, spot):
+        if isinstance(array, tuple):
+            return array[spot[0]].at[spot[1:]] if len(spot) > 1 else array[spot[0]]
+        return array.at[spot]
+
+    for k, pieces in enumerate(loads):
+        for array, spot, inside in pieces:
+            pltpu.make_async_copy(place(array, spot), grad_buf.at[(k,) + inside], load_sem.at[k]).start()
+
+    def before(k):
+        pltpu.make_async_copy(grad_buf.at[k], grad_buf.at[k], load_sem.at[k]).wait()
+
+    def after(k):
+        for num, pieces in enumerate(stores):
+            @pl.when(k == num)
+            def _():
+                for array, spot, inside in pieces:
+                    pltpu.make_async_copy(full_buf.at[(num,) + inside], place(array, spot), out_sem.at[num]).start()
+
+    all_reduce_body(CHUNKS, *bufs, before, after)
+    for k in range(CHUNKS):
+        pltpu.make_async_copy(full_buf.at[k], full_buf.at[k], out_sem.at[k]).wait()
+
+
+def reduce_grads(ups_one, downs_one, merge, ups_two, downs_two, head):
+    any_hbm = pl.BlockSpec(memory_space=pltpu.HBM)
+    shapes = ((4, 128, 512), (4, 512, 128), (512, 512), (3, 512, 2048), (3, 2048, 512), (512, 1024))
+    return pl.pallas_call(
+        reduce_kernel,
+        out_shape=[jax.ShapeDtypeStruct(shape, jnp.bfloat16) for shape in shapes],
+        in_specs=[any_hbm] * 16,
+        out_specs=[any_hbm] * 6,
+        scratch_shapes=[pltpu.SemaphoreType.DMA((CHUNKS,)), pltpu.SemaphoreType.DMA((CHUNKS,))] + scratch(CHUNKS, 512),
+        compiler_params=pltpu.CompilerParams(has_side_effects=True, vmem_limit_bytes=52 * 2**20),
+        cost_estimate=pl.CostEstimate(flops=10**9, bytes_accessed=3 * 10**7, transcendentals=0),
+    )(*ups_one, *downs_one, merge, *ups_two, *downs_two, head)
+
+
 def solution(mesh):
     data_devs = mesh.shape['data']
 
@@ -124,23 +389,24 @@
         logits, saved = model_forward(x_now, weights)
         saved_one, merged, saved_two, head_in_b, head_back = saved
         grad_logits = loss_grad(logits, labels_now, img_count * data_devs)
-        sum_head = lax.psum(contract_rows(head_in_b, grad_logits).astype(jnp.bfloat16), 'data')
+        sum_head = contract_rows(head_in_b, jnp.pad(grad_logits, ((0, 0), (0, 24)))).astype(jnp.bfloat16)
         grad_resid = head_input_grad(grad_logits, head_w, head_back, tokens // 4)
         sums_up_two = [None] * depth_two
         sums_down_two = [None] * depth_two
         for layer_num in reversed(range(depth_two)):
             grad_resid, grad_up, grad_down = block_backward(grad_resid, saved_two[layer_num], ups_two[layer_num], downs_two[layer_num])
-            sums_down_two[layer_num] = lax.psum(grad_down.astype(jnp.bfloat16), 'data')
-            sums_up_two[layer_num] = lax.psum(grad_up.astype(jnp.bfloat16), 'data')
-        sum_merge = lax.psum(contract_rows(merged, grad_resid).astype(jnp.bfloat16), 'data')
+            sums_down_two[layer_num] = grad_down.astype(jnp.bfloat16)
+            sums_up_two[layer_num] = grad_up.astype(jnp.bfloat16)
+        sum_merge = contract_rows(merged, grad_resid).astype(jnp.bfloat16)
         grad_resid = contract_cols(grad_resid, merge_w).astype(jnp.bfloat16).reshape(img_count * tokens, width)
         sums_up_one = [None] * depth_one
         sums_down_one = [None] * depth_one
         for layer_num in reversed(range(depth_one)):
             grad_resid, grad_up, grad_down = block_backward(grad_resid, saved_one[layer_num], ups_one[layer_num], downs_one[layer_num])
-            sums_down_one[layer_num] = lax.psum(grad_down.astype(jnp.bfloat16), 'data')
-            sums_up_one[layer_num] = lax.psum(grad_up.astype(jnp.bfloat16), 'data')
-        grad_sums = (jnp.stack(sums_up_one), jnp.stack(sums_down_one), sum_merge, jnp.stack(sums_up_two), jnp.stack(sums_down_two), sum_head)
+            sums_down_one[layer_num] = grad_down.astype(jnp.bfloat16)
+            sums_up_one[layer_num] = grad_up.astype(jnp.bfloat16)
+        grad_sums = reduce_grads(sums_up_one, sums_down_one, sum_merge, sums_up_two, sums_down_two, sum_head)
+        grad_sums = tuple(grad_sums[:5]) + (grad_sums[5][:, :1000],)
         return finish_step(params, velocities, grad_sums, x_next)
 
     replicated = P()

time: 818 us -> 405 us (0.50)
  waiting for transfers between devices: 517 us -> 0 us
  Pallas kernels: 0 us -> 128 us
  matrix products: 134 us -> 116 us
  between operations: 18.1 us -> 5.43 us
    psum x1 -> x0, waiting for transfers between devices: 517 us -> none  [local_step(): lax.psum(contract_rows(head_in_b, grad_logits).astype(jnp.bfloat16), 'data')]
    pallas_call x0 -> x1, Pallas kernels: none -> 128 us  [reduce_grads(): pl.pallas_call(reduce_kernel, out_shape=[jax.ShapeDtypeStruct(shape, jnp....]
    unnamed x130 -> x216, local copies, waits for them, and re-layouts: 9.59 us -> 23 us
    dot_general x14, matrix products: 49.5 us -> 39.3 us  [block_forward(): block_out = jnp.dot(activated_b, w_down, preferred_element_type=jnp.float32)]
  transfers between devices with their start and end apart: 1 -> 0, of which waited for: 1 -> 0; matrix products, arithmetic and copies ran while one was open for 0% -> 0% of each run, Pallas kernels for 0% -> 0%
where the time goes in v1:
time: 405 us; the launch traced here: 398 us
  Pallas kernels  128 us (32%)
  other arithmetic  120 us (30%)
  matrix products  116 us (29%)
  local copies, waits for them, and re-layouts  27.7 us (7%)
  between operations  5.43 us (1%)
    pallas_call x1, Pallas kernels, reduce_grads(): pl.pallas_call(reduce_kernel, out_shape=[jax.ShapeDtypeStruct(shape, jnp....  128 us
    another operation x4, other arithmetic  47.4 us
    dot_general x14, matrix products, block_forward(): block_out = jnp.dot(activated_b, w_down, preferred_element_type=jnp.float32)  39.3 us
    dot_general x16, matrix products, contract_rows(): lax.dot_general(lhs_mat, rhs_mat, (((0,), (0,)), ((), ())), preferred_ele...  36.2 us
    reduce_sum x6, other arithmetic, lars_step(): w_norm = jnp.sqrt(jnp.sum(weight * weight, axis=red_axes, keepdims=True))  30.1 us
    dot_general x14, matrix products, contract_cols(): lax.dot_general(lhs_mat, rhs_mat, (((1,), (1,)), ((), ())), preferred_ele...  26.2 us
    unnamed x216, local copies, waits for them, and re-layouts  23 us
    reduce_sum x6, other arithmetic, lars_step(): g_norm = jnp.sqrt(jnp.sum(grad_f * grad_f, axis=red_axes, keepdims=True))  12.2 us

profile of v1, /device:TPU:0, one launch (start us, length us, event | category | flops | bytes accessed | tf_op | source)
XLA Modules:
  0.0 397.6 jit_solution(6320614154765370345)
XLA Ops:
  0.7 2.3 multiply_reduce_fusion.5
  4.4 1.6 multiply_reduce_fusion.24
  16.9 3.0 multiply_convert_fusion.3
  24.5 11.1 %multiply_reduce_fusion.1 = (f32[3]{0:T(128)}, bf16[3,512,2048]{2,1,0:T(8,128)(2,1)S(1)}) fusion(f32[3,512,2048]{2,1,0:T(8,128)} %param.21), kind=kLoop, calls=%fused_computation.9 | loop fusion | flops 9437181 | bytes 18874380 | tf_op jit(solution)/shard_map/reduce_sum | solution.py:103
  35.6 4.5 %fusion.133 = f32[392,2048]{1,0:T(8,128)} fusion(bf16[3,512,2048]{2,1,0:T(8,128)(2,1)S(1)} %get-tuple-element.84, f32[392,512]{1,0:T(8,128)} %copy-done.13, f32[392]{0:T(512)} %fusion.226, f32[392]{0:T(512)} %copy-done.66), kind=kOutput, calls=%fused_computation.196 | convolution fusion | flops 822685696 | bytes 6114368 | tf_op jit(solution)/shard_map/dot_general | solution.py:46
  40.0 13.7 %multiply_reduce_fusion = (f32[3]{0:T(128)}, bf16[3,2048,512]{2,1,0:T(8,128)(2,1)}) fusion(f32[3,2048,512]{2,1,0:T(8,128)} %param.22), kind=kLoop, calls=%fused_computation.8 | loop fusion | flops 9437181 | bytes 18874380 | tf_op jit(solution)/shard_map/reduce_sum | solution.py:103
  53.8 4.0 %fusion.289 = (f32[392]{0:T(512)S(1)}, f32[392,512]{1,0:T(8,128)S(1)}) fusion(f32[392,512]{1,0:T(8,128)} %copy-done.13, bf16[3,2048,512]{2,1,0:T(8,128)(2,1)} %get-tuple-element.86, f32[392,2048]{1,0:T(8,128)} %fusion.133), kind=kOutput, calls=%fused_computation.479 | convolution fusion | flops 830111360 | bytes 6915616 | tf_op jit(solution)/shard_map/dot_general | solution.py:49
  60.3 4.1 %fusion.290 = (f32[392]{0:T(512)S(1)}, f32[392,512]{1,0:T(8,128)S(1)}) fusion(f32[392,512]{1,0:T(8,128)S(1)} %get-tuple-element.102, bf16[3,2048,512]{2,1,0:T(8,128)(2,1)} %get-tuple-element.86, f32[392,2048]{1,0:T(8,128)S(1)} %fusion.137), kind=kOutput, calls=%fused_computation.480 | convolution fusion | flops 830111360 | bytes 6915616 | tf_op jit(solution)/shard_map/dot_general | solution.py:49
  67.0 1.7 copy-done.29
  68.7 4.8 %fusion.149 = f32[392,512]{1,0:T(8,128)} fusion(f32[392,512]{1,0:T(8,128)S(1)} %get-tuple-element.104, f32[3,2048,512]{2,1,0:T(8,128)} %param.22, f32[392,2048]{1,0:T(8,128)S(1)} %fusion.141), kind=kOutput, calls=%fused_computation.221 | convolution fusion | flops 829911040 | bytes 6914048 | tf_op jit(solution)/shard_map/dot_general | solution.py:49
  76.1 1.5 convolution_convert_fusion.6.refs_15_
  78.5 5.0 %convolution_convert_fusion.refs_14_ = bf16[2048,512]{1,0:T(8,128)(2,1)} fusion(bf16[392,512]{1,0:T(8,128)(2,1)S(1)} %reshape.474, f32[392,2048]{1,0:T(8,128)} %copy-done.29), kind=kOutput, calls=%fused_computation.144 | convolution fusion | flops 830357504 | bytes 5709824 | tf_op jit(solution)/shard_map/dot_general | solution.py:27
  83.5 4.9 %fusion.52 = bf16[392,2048]{1,0:T(8,128)(2,1)S(1)} fusion(f32[392,2048]{1,0:T(8,128)S(1)} %copy-done.30, bf16[392,512]{1,0:T(8,128)(2,1)S(1)} %reshape.474, f32[3,2048,512]{2,1,0:T(8,128)} %param.22), kind=kOutput, calls=%fused_computation.80 | convolution fusion | flops 838139904 | bytes 7315456 | tf_op jit(solution)/shard_map/dot_general | solution.py:31
  91.5 2.9 convolution_convert_fusion.1.refs_13_
  94.4 2.9 fusion.45
  100.5 2.8 convolution_convert_fusion.2.refs_12_
  103.3 2.8 convolution_convert_fusion.3.refs_11_
  106.1 2.8 convolution_convert_fusion.4.refs_10_
  108.8 2.7 fusion.38
  111.6 2.7 convolution_convert_fusion.5.refs_9_
  119.1 4.4 %fusion.31 = bf16[1568,512]{1,0:T(8,128)(2,1)S(1)} fusion(f32[1568,512]{1,0:T(8,128)} %get-tuple-element.98, bf16[1568,128]{1,0:T(8,128)(2,1)S(1)} %reshape.475, f32[4,512,128]{2,1,0:T(8,128)} %param.19), kind=kOutput, calls=%fused_computation.59 | convolution fusion | flops 221577216 | bytes 5349376 | tf_op jit(solution)/shard_map/dot_general | solution.py:31
  128.0 2.5 fusion.24
  134.5 2.5 fusion.17
  138.8 1.6 fusion.278
  140.6 2.7 fusion.172
  144.1 3.4 convolution_convert_fusion.14.refs_4_
  150.8 4.5 %fusion.162.refs_0_ = bf16[128,512]{1,0:T(8,128)(2,1)S(1)} fusion(bf16[1568,128]{1,0:T(8,128)(2,1)S(1)} %copy-done.58, f32[1568,512]{1,0:T(8,128)} %copy-done.38, bf16[1568,128]{1,0:T(8,128)(2,1)S(1)} %copy-done.60, bf16[4,512,128]{2,1,0:T(8,128)(2,1)} %copy-done.54), kind=kOutput, calls=%fused_computation.243 | convolution fusion | flops 427163648 | bytes 4276224 | tf_op jit(solution)/shard_map/dot_general | solution.py:27
  155.3 128.5 %shard_map.246 = (bf16[4,128,512]{2,1,0:T(8,128)(2,1)S(1)}, bf16[4,512,128]{2,1,0:T(8,128)(2,1)}, bf16[512,512]{1,0:T(8,128)(2,1)}, bf16[3,512,2048]{2,1,0:T(8,1...) custom-call(bf16[128,512]{1,0:T(8,128)(2,1)S(1)} %fusion.162.refs_0_, ...), custom_call_target="tpu_custom_call" | custom-call | flops 1000000000 | bytes 30000000 | tf_op jit(solution)/shard_map/pallas_call | solution.py:367
  283.8 1.9 fusion.167
  288.0 3.1 fusion.270
  291.3 3.4 fusion.272
  295.0 1.7 fusion.274
  300.0 1.6 fusion.293
  302.2 1.6 fusion.294
  304.3 2.6 fusion.122
  308.8 4.4 %fusion = f32[3]{0:T(128)S(1)} fusion(bf16[3,512,2048]{2,1,0:T(8,128)(2,1)} %get-tuple-element.22), kind=kLoop, calls=%fused_computation.4 | loop fusion | flops 9437181 | bytes 6291468 | tf_op jit(solution)/shard_map/reduce_sum | solution.py:104
  313.2 24.7 %fusion.266 = (bf16[3,512,2048]{2,1,0:T(8,128)(2,1)}, f32[3,512,2048]{2,1,0:T(8,128)}, f32[3,512,2048]{2,1,0:T(8,128)}) fusion(f32[3,512,2048]{2,1,0:T(8,128)} %param.21, bf16[3,512,2048]{2,1,0:T(8,128)(2,1)} %get-tuple-element.22, f32[3]{0:T(128)S(1)} %multiply_multiply_fusion.28, f32[3,512,2048]{2,1,0:T(8,128)} %param.27), kind=kLoop, calls=%fused_computation.462 | loop fusion | flops 18874368 | bytes 62914572 | tf_op jit(solution)/shard_map/convert.9
  337.9 4.4 %fusion.2 = f32[3]{0:T(128)S(1)} fusion(bf16[3,2048,512]{2,1,0:T(8,128)(2,1)} %get-tuple-element.23), kind=kLoop, calls=%fused_computation.6 | loop fusion | flops 9437181 | bytes 6291468 | tf_op jit(solution)/shard_map/reduce_sum | solution.py:104
  342.3 17.6 %fusion.268 = (bf16[3,2048,512]{2,1,0:T(8,128)(2,1)}, f32[3,2048,512]{2,1,0:T(8,128)}, f32[3,2048,512]{2,1,0:T(8,128)}) fusion(f32[3,2048,512]{2,1,0:T(8,128)S(1)} %bitcast.243, bf16[3,2048,512]{2,1,0:T(8,128)(2,1)} %get-tuple-element.23, f32[3]{0:T(128)S(1)} %multiply_multiply_fusion.27, f32[3,2048,512]{2,1,0:T(8,128)} %param.28), kind=kLoop, calls=%fused_computation.463 | loop fusion | flops 18874368 | bytes 62914572 | tf_op jit(solution)/shard_map/convert.8
  360.0 4.6 %fusion.296 = (f32[392]{0:T(512)S(1)}, f32[392,512]{1,0:T(8,128)S(1)}) fusion(f32[392,512]{1,0:T(8,128)S(1)} %copy-done.40, bf16[3,2048,512]{2,1,0:T(8,128)(2,1)} %get-tuple-element.54, bf16[3,512,2048]{2,1,0:T(8,128)(2,1)} %get-tuple-element.51, f32[392]{0:T(512)S(1)} %add_rsqrt_fusion.7, f32[392]{0:T(512)S(1)} %broadcast_multiply_fusion.10), kind=kOutput, calls=%fused_computation.486 | convolution fusion | flops 1652797056 | bytes 6608416 | tf_op jit(solution)/shard_map/dot_general | solution.py:49
  364.8 4.6 %fusion.297 = (f32[392]{0:T(512)S(1)}, f32[392,512]{1,0:T(8,128)S(1)}) fusion(f32[392,512]{1,0:T(8,128)S(1)} %get-tuple-element.130, bf16[3,2048,512]{2,1,0:T(8,128)(2,1)} %get-tuple-element.54, bf16[3,512,2048]{2,1,0:T(8,128)(2,1)} %get-tuple-element.51, f32[392]{0:T(512)S(1)} %add_rsqrt_fusion.6, f32[392]{0:T(512)S(1)} %broadcast_multiply_fusion.9), kind=kOutput, calls=%fused_computation.487 | convolution fusion | flops 1652797056 | bytes 6608416 | tf_op jit(solution)/shard_map/dot_general | solution.py:49
  369.7 5.5 %fusion.151 = f32[392,512]{1,0:T(8,128)} fusion(f32[392,512]{1,0:T(8,128)S(1)} %get-tuple-element.132, bf16[3,2048,512]{2,1,0:T(8,128)(2,1)} %get-tuple-element.54, bf16[3,512,2048]{2,1,0:T(8,128)(2,1)} %get-tuple-element.51, f32[392]{0:T(512)S(1)} %add_rsqrt_fusion.5, f32[392]{0:T(512)S(1)} %broadcast_multiply_fusion.8), kind=kOutput, calls=%fused_computation.223 | convolution fusion | flops 1652596736 | bytes 6606848 | tf_op jit(solution)/shard_map/dot_general | solution.py:49
  375.2 2.3 reshape.480
  382.7 2.9 copy.32
  385.6 1.8 copy.33
  387.4 4.3 %fusion.276 = (f32[512,1000]{1,0:T(8,128)S(1)}, f32[512,1000]{1,0:T(8,128)}) fusion(f32[512,1000]{1,0:T(8,128)} %copy.33, bf16[512,1024]{1,0:T(8,128)(2,1)S(1)} %copy-done.34, f32[]{:T(128)S(6)} %mul.1125, f32[512,1000]{1,0:T(8,128)} %copy.32), kind=kLoop, calls=%fused_computation.467 | loop fusion | flops 2560000 | bytes 9216004 | tf_op jit(solution)/shard_map/sub | solution.py:106
  392.6 1.8 copy.34
  394.4 2.9 copy.35
  (344 shorter events, 62.7 us)
Async XLA Ops:
  0.6 7.5 %copy-start.31 = (f32[4,512,128]{2,1,0:T(8,128)S(1)}, f32[4,512,128]{2,1,0:T(8,128)}, u32[]{:S(2)}) copy-start(f32[4,512,128]{2,1,0:T(8,128)} %param.19) | copy-start | bytes 3145732
  3.0 13.9 %copy-start.36 = (bf16[4,128,512]{2,1,0:T(8,128)(2,1)}, bf16[4,128,512]{2,1,0:T(8,128)(2,1)S(1)}, u32[]{:S(2)}) copy-start(bf16[4,128,512]{2,1,0:T(8,128)(2,1)S(1)} %get-tuple-element.88) | copy-start | bytes 1572868
  4.4 4.7 %copy-start.64 = (f32[2,784]{1,0:T(2,128)}, f32[2,784]{1,0:T(2,128)S(1)}, u32[]{:S(2)}) copy-start(f32[2,784]{1,0:T(2,128)S(1)} %broadcast_multiply_fusion.6) | copy-start | bytes 18820
  4.4 4.7 %copy-start.25 = (bf16[2,784,128]{2,1,0:T(8,128)(2,1)S(1)}, bf16[2,784,128]{2,1,0:T(8,128)(2,1)}, u32[]{:S(2)}) copy-start(bf16[2,784,128]{2,1,0:T(8,128)(2,1)} %param.15) | copy-start | bytes 1204228
  6.1 4.4 %copy-start.86 = (f32[2,784]{1,0:T(2,128)}, f32[2,784]{1,0:T(2,128)S(1)}, u32[]{:S(2)}) copy-start(f32[2,784]{1,0:T(2,128)S(1)} %add_rsqrt_fusion.3) | copy-start | bytes 18820
  9.1 5.4 %copy-start.54 = (bf16[4,512,128]{2,1,0:T(8,128)(2,1)}, bf16[4,512,128]{2,1,0:T(8,128)(2,1)S(1)}, u32[]{:S(2)}) copy-start(bf16[4,512,128]{2,1,0:T(8,128)(2,1)S(1)} %get-tuple-element.90) | copy-start | bytes 1572868
  16.3 3.6 copy-start.3
  16.8 3.0 copy-start.84
  16.9 3.0 copy-start.77
  35.6 29.8 %copy-start.2 = (bf16[3,512,2048]{2,1,0:T(8,128)(2,1)}, bf16[3,512,2048]{2,1,0:T(8,128)(2,1)S(1)}, u32[]{:S(2)}) copy-start(bf16[3,512,2048]{2,1,0:T(8,128)(2,1)S(1)} %get-tuple-element.84) | copy-start | bytes 18874372
  60.3 4.1 %copy-start.27 = (f32[392,2048]{1,0:T(8,128)}, f32[392,2048]{1,0:T(8,128)S(1)}, u32[]{:S(2)}) copy-start(f32[392,2048]{1,0:T(8,128)S(1)} %fusion.137) | copy-start | bytes 9633796
  78.4 10.0 %slice-start.3 = ((s8[6291456]{0:T(1024)(128)(4,1)}), s8[2097152]{0:T(1024)(128)(4,1)S(1)}, s32[]{:S(2)}) async-start(s8[6291456]{0:T(1024)(128)(4,1)} %bitcast.244), calls=%async_computation.3 | async-start | bytes 4194304
  78.5 5.0 %copy-start.51 = (bf16[392,512]{1,0:T(8,128)(2,1)}, bf16[392,512]{1,0:T(8,128)(2,1)S(1)}, u32[]{:S(2)}) copy-start(bf16[392,512]{1,0:T(8,128)(2,1)S(1)} %reshape.474) | copy-start | bytes 1204228
  78.5 5.0 %copy-start.30 = (f32[392,2048]{1,0:T(8,128)S(1)}, f32[392,2048]{1,0:T(8,128)}, u32[]{:S(2)}) copy-start(f32[392,2048]{1,0:T(8,128)} %copy-done.29) | copy-start | bytes 9633796
  78.5 9.9 %slice-start.4 = ((s8[6291456]{0:T(1024)(128)(4,1)}), s8[4194304]{0:T(1024)(128)(4,1)S(1)}, s32[]{:S(2)}) async-start(s8[6291456]{0:T(1024)(128)(4,1)} %bitcast.244), calls=%async_computation.4 | async-start | bytes 8388608
  83.5 4.9 %copy-start.18 = (f32[392,512]{1,0:T(8,128)S(1)}, f32[392,512]{1,0:T(8,128)}, u32[]{:S(2)}) copy-start(f32[392,512]{1,0:T(8,128)} %copy-done.17) | copy-start | bytes 2408452
  83.5 4.9 %copy-start.71 = (f32[392]{0:T(512)S(1)}, f32[392]{0:T(512)}, u32[]{:S(2)}) copy-start(f32[392]{0:T(512)} %copy-done.70) | copy-start | bytes 4708
  90.0 4.4 %slice-start.5 = ((s8[6291456]{0:T(1024)(128)(4,1)}), s8[4194304]{0:T(1024)(128)(4,1)S(1)}, s32[]{:S(2)}) async-start(s8[6291456]{0:T(1024)(128)(4,1)} %bitcast.247), calls=%async_computation.5 | async-start | bytes 8388608
  94.4 3.0 copy-start.69
  118.4 5.1 %copy-start.50 = (bf16[1568,128]{1,0:T(8,128)(2,1)}, bf16[1568,128]{1,0:T(8,128)(2,1)S(1)}, u32[]{:S(2)}) copy-start(bf16[1568,128]{1,0:T(8,128)(2,1)S(1)} %reshape.475) | copy-start | bytes 1204228
  119.1 4.4 %copy-start.4 = (f32[1568,128]{1,0:T(8,128)S(1)}, f32[1568,128]{1,0:T(8,128)}, u32[]{:S(2)}) copy-start(f32[1568,128]{1,0:T(8,128)} %copy-done.3) | copy-start | bytes 2408452
  119.1 4.4 %copy-start.37 = (bf16[4,128,512]{2,1,0:T(8,128)(2,1)S(1)}, bf16[4,128,512]{2,1,0:T(8,128)(2,1)}, u32[]{:S(2)}) copy-start(bf16[4,128,512]{2,1,0:T(8,128)(2,1)} %copy-done.36) | copy-start | bytes 1572868
  123.6 3.0 copy-start.19
  123.6 3.0 copy-start.44
  134.5 3.6 copy-start.6
  144.1 3.5 copy-start.20
  144.1 3.5 copy-start.79
  144.1 4.6 %copy-start.9 = (f32[1568,128]{1,0:T(8,128)S(1)}, f32[1568,128]{1,0:T(8,128)}, u32[]{:S(2)}) copy-start(f32[1568,128]{1,0:T(8,128)} %copy-done.7) | copy-start | bytes 2408452
  144.1 4.6 %copy-start.22 = (bf16[1568,512]{1,0:T(8,128)(2,1)S(1)}, bf16[1568,512]{1,0:T(8,128)(2,1)}, u32[]{:S(2)}) copy-start(bf16[1568,512]{1,0:T(8,128)(2,1)} %copy-done.21) | copy-start | bytes 4816900
  144.1 4.6 %copy-start.63 = (f32[1568]{0:T(1024)S(1)}, f32[1568]{0:T(1024)}, u32[]{:S(2)}) copy-start(f32[1568]{0:T(1024)} %copy-done.61) | copy-start | bytes 18820
  147.6 3.2 copy-start.58
  147.6 3.2 copy-start.60
  155.3 131.1 %copy-start.12 = (f32[512,512]{1,0:T(8,128)S(1)}, f32[512,512]{1,0:T(8,128)}, u32[]{:S(2)}) copy-start(f32[512,512]{1,0:T(8,128)} %param.20) | copy-start | bytes 3145732
  285.7 5.6 %copy-start.96 = (f32[4]{0:T(128)S(1)}, f32[4]{0:T(128)}, u32[]{:S(2)}) copy-start(f32[4]{0:T(128)} %get-tuple-element.87) | copy-start | bytes 52
  291.1 3.7 copy-start.45
  291.1 3.9 copy-start.97
  291.1 3.9 copy-start.32
  291.1 4.0 copy-start.53
  294.8 7.4 %copy-start.56 = (bf16[4,128,512]{2,1,0:T(8,128)(2,1)}, bf16[4,128,512]{2,1,0:T(8,128)(2,1)S(1)}, u32[]{:S(2)}) copy-start(bf16[4,128,512]{2,1,0:T(8,128)(2,1)S(1)} %get-tuple-element.59) | copy-start | bytes 1572868
  296.7 5.5 %copy-start.57 = (bf16[4,512,128]{2,1,0:T(8,128)(2,1)}, bf16[4,512,128]{2,1,0:T(8,128)(2,1)S(1)}, u32[]{:S(2)}) copy-start(bf16[4,512,128]{2,1,0:T(8,128)(2,1)S(1)} %get-tuple-element.62) | copy-start | bytes 1572868
  308.8 4.4 %copy-start.95 = (f32[3]{0:T(128)S(1)}, f32[3]{0:T(128)}, u32[]{:S(2)}) copy-start(f32[3]{0:T(128)} %get-tuple-element.83) | copy-start | bytes 40
  313.2 29.1 %slice-start = ((s8[12582912]{0:T(1024)(128)(4,1)}), s8[4194304]{0:T(1024)(128)(4,1)S(1)}, s32[]{:S(2)}) async-start(s8[12582912]{0:T(1024)(128)(4,1)} %bitcast.242), calls=%async_computation | async-start | bytes 8388608
  313.2 29.1 %slice-start.1 = ((s8[12582912]{0:T(1024)(128)(4,1)}), s8[4194304]{0:T(1024)(128)(4,1)S(1)}, s32[]{:S(2)}) async-start(s8[12582912]{0:T(1024)(128)(4,1)} %bitcast.242), calls=%async_computation.1 | async-start | bytes 8388608
  313.2 29.1 %slice-start.2 = ((s8[12582912]{0:T(1024)(128)(4,1)}), s8[4194304]{0:T(1024)(128)(4,1)S(1)}, s32[]{:S(2)}) async-start(s8[12582912]{0:T(1024)(128)(4,1)} %bitcast.242), calls=%async_computation.2 | async-start | bytes 8388608
  337.9 4.4 %copy-start.94 = (f32[3]{0:T(128)S(1)}, f32[3]{0:T(128)}, u32[]{:S(2)}) copy-start(f32[3]{0:T(128)} %get-tuple-element.85) | copy-start | bytes 40
  342.3 17.7 %copy-start.40 = (f32[392,512]{1,0:T(8,128)S(1)}, f32[392,512]{1,0:T(8,128)}, u32[]{:S(2)}) copy-start(f32[392,512]{1,0:T(8,128)} %copy-done.39) | copy-start | bytes 2408452
  369.7 9.3 %copy-start.34 = (bf16[512,1024]{1,0:T(8,128)(2,1)S(1)}, bf16[512,1024]{1,0:T(8,128)(2,1)}, u32[]{:S(2)}) copy-start(bf16[512,1024]{1,0:T(8,128)(2,1)} %get-tuple-element.24) | copy-start | bytes 3145732
  375.2 5.6 %copy-start.1 = (f32[512,1000]{0,1:T(8,128)S(1)}, f32[512,1000]{0,1:T(8,128)}, u32[]{:S(2)}) copy-start(f32[512,1000]{0,1:T(8,128)} %param.23) | copy-start | bytes 6144004
  (58 other events, 95.7 us)

commit v2 on v1

v2 whole, which is shorter than its diff:
```python
import functools

import jax
import jax.numpy as jnp
from jax import lax
from jax.experimental import pallas as pl
from jax.experimental.pallas import tpu as pltpu
from jax.sharding import PartitionSpec as P

MOMENTUM = 0.9
TRUST = 0.1
LN_EPS = 1e-6
CHUNKS = 29
HEAD_A, HEAD_B, MERGE, DOWN_ONE, UP_ONE = 24, 25, 26, 27, 28
HEAD_REST = 488
CLASSES = 1000
LANES = 512
RING = 8
AHEAD = 4
W_RING = 3
TOKENS_TWO = 196
PAD_IMG = 208
PAD_ROWS = 416
GELU_C = 0.7978845608028654
GELU_A = 0.044715
WIDE = 512
THIN = 128
STEP = 32
QUARTER = 64
HALF = 256
TWO_CHUNKS = 24
OCT = 8
PAIR = 16

MESH = pl.DeviceIdType.MESH
ROWS = WIDE
LAG = 3
STAGES = 12


def all_reduce_body(chunks, grad_buf, full_buf, recv_core, recv_one, recv_z, recv_mid, recv_two, send_sem, recv_sem, before, after, extra):
    me = lax.axis_index('data')
    core = me % 2
    x_pos = (me // 2) % 2
    y_pos = (me // 4) % 2
    z_pos = me // OCT
    one = x_pos * (1 - core) + y_pos * core
    two = y_pos * (1 - core) + x_pos * core
    one_step = 2 * (1 - core) + 4 * core
    two_step = 4 * (1 - core) + 2 * core
    dev_core = me + 1 - 2 * core
    dev_one = me + one_step * (1 - 2 * one)
    dev_two = me + two_step * (1 - 2 * two)
    upper = z_pos // 2
    is_end = (z_pos % 3) == 0
    is_mid = (z_pos % 3) != 0
    dev_inner = me + OCT * (1 - 2 * upper)
    dev_outer = me - OCT * (1 - 2 * upper)
    half = core * HALF
    quarter = half + one * THIN
    near = quarter + upper * QUARTER
    far = quarter + (1 - upper) * QUARTER
    mine = near + two * STEP

    def rows(chunk, start, size):
        return grad_buf.at[chunk, pl.ds(pl.multiple_of(start, STEP), size)]

    def full(chunk, start, size):
        return full_buf.at[chunk, pl.ds(pl.multiple_of(start, STEP), size)]

    def remote(src, dst, which, chunk, dev):
        return pltpu.make_async_remote_copy(src_ref=src, dst_ref=dst, send_sem=send_sem.at[which, chunk], recv_sem=recv_sem.at[which, chunk], device_id=(dev,), device_id_type=MESH)

    def add_in(chunk, start, size, recv):
        def step(num, carry):
            spot = pl.ds(pl.multiple_of(start + num * STEP, STEP), STEP)
            grad_buf[chunk, spot, :] = grad_buf[chunk, spot, :] + recv[chunk, pl.ds(pl.multiple_of(num * STEP, STEP), STEP), :]
            return carry
        lax.fori_loop(0, size // STEP, step, 0)

    def c_core(k):
        return remote(rows(k, HALF - half, HALF), recv_core.at[k], 0, k, dev_core)

    def c_one(k):
        return remote(rows(k, half + (1 - one) * THIN, THIN), recv_one.at[k], 1, k, dev_one)

    def c_in(k):
        return remote(rows(k, far, QUARTER), recv_z.at[k], 2, k, dev_inner)

    def c_mid(k):
        return remote(rows(k, far, QUARTER), recv_mid.at[k], 3, k, dev_inner)

    def c_out(k):
        return remote(rows(k, near, QUARTER), recv_z.at[k], 2, k, dev_outer)

    def c_two(k):
        return remote(rows(k, near + (1 - two) * STEP, STEP), recv_two.at[k], 4, k, dev_two)

    def g_two(k):
        return remote(full(k, mine, STEP), full(k, mine, STEP), 5, k, dev_two)

    def g_in(k):
        return remote(full(k, near, QUARTER), full(k, near, QUARTER), 6, k, dev_inner)

    def g_mid(k):
        return remote(full(k, near, QUARTER), full(k, near, QUARTER), 7, k, dev_inner)

    def g_out(k):
        return remote(full(k, far, QUARTER), full(k, far, QUARTER), 6, k, dev_outer)

    def g_one(k):
        return remote(full(k, quarter, THIN), full(k, quarter, THIN), OCT, k, dev_one)

    def g_core(k):
        return remote(full(k, half, HALF), full(k, half, HALF), 9, k, dev_core)

    def stage_0(k):
        before(k)
        c_core(k).start()

    def stage_1(k):
        c_core(k).wait()
        add_in(k, half, HALF, recv_core)
        c_one(k).start()

    def stage_2(k):
        c_one(k).wait()
        add_in(k, quarter, THIN, recv_one)
        @pl.when(is_end)
        def _():
            c_in(k).start()

    def stage_3(k):
        @pl.when(is_end)
        def _():
            c_in(k).wait_send()
        @pl.when(is_mid)
        def _():
            c_out(k).wait_recv()
            add_in(k, far, QUARTER, recv_z)
            c_mid(k).start()

    def stage_4(k):
        @pl.when(is_mid)
        def _():
            c_mid(k).wait()
            add_in(k, near, QUARTER, recv_mid)
            c_out(k).start()

    def stage_5(k):
        @pl.when(is_mid)
        def _():
            c_out(k).wait_send()
        @pl.when(is_end)
        def _():
            c_in(k).wait_recv()
            add_in(k, near, QUARTER, recv_z)
            c_two(k).start()

    def stage_6(k):
        @pl.when(is_end)
        def _():
            c_two(k).wait()
            spot = pl.ds(pl.multiple_of(mine, STEP), STEP)
            full_buf[k, spot, :] = grad_buf[k, spot, :] + recv_two[k]
            g_two(k).start()

    def stage_7(k):
        @pl.when(is_end)
        def _():
            g_two(k).wait()
            g_in(k).start()

    def stage_8(k):
        @pl.when(is_end)
        def _():
            g_in(k).wait_send()
        @pl.when(is_mid)
        def _():
            g_out(k).wait_recv()
            g_mid(k).start()

    def stage_9(k):
        @pl.when(is_mid)
        def _():
            g_mid(k).wait()
            g_out(k).start()

    def stage_10(k):
        @pl.when(is_mid)
        def _():
            g_out(k).wait_send()
        @pl.when(is_end)
        def _():
            g_in(k).wait_recv()
        g_one(k).start()

    def stage_11(k):
        g_one(k).wait()
        g_core(k).start()

    def stage_12(k):
        g_core(k).wait()
        after(k)

    stages = (stage_0, stage_1, stage_2, stage_3, stage_4, stage_5, stage_6, stage_7, stage_8, stage_9, stage_10, stage_11, stage_12)

    def tick(t, carry):
        for num, stage in enumerate(stages):
            k = t - num * LAG
            pl.when((k >= 0) & (k < chunks))(functools.partial(stage, k))
        extra(t)
        return carry

    lax.fori_loop(0, chunks + STAGES * LAG, tick, 0)


def scratch(chunks, cols):
    return [
        pltpu.VMEM((chunks, WIDE, cols), jnp.bfloat16),
        pltpu.VMEM((chunks, WIDE, cols), jnp.bfloat16),
        pltpu.VMEM((chunks, HALF, cols), jnp.bfloat16),
        pltpu.VMEM((chunks, THIN, cols), jnp.bfloat16),
        pltpu.VMEM((chunks, QUARTER, cols), jnp.bfloat16),
        pltpu.VMEM((chunks, QUARTER, cols), jnp.bfloat16),
        pltpu.VMEM((chunks, STEP, cols), jnp.bfloat16),
        pltpu.SemaphoreType.DMA((10, chunks)),
        pltpu.SemaphoreType.DMA((10, chunks)),
    ]


def layer_norm(values):
    row_mean = jnp.mean(values, axis=-1, keepdims=True)
    centered = values - row_mean
    variance = jnp.mean(centered * centered, axis=-1, keepdims=True)
    return centered * lax.rsqrt(variance + LN_EPS)


def layer_norm_parts(values):
    row_mean = jnp.mean(values, axis=-1, keepdims=True)
    centered = values - row_mean
    variance = jnp.mean(centered * centered, axis=-1, keepdims=True)
    inverse = lax.rsqrt(variance + LN_EPS)
    return centered * inverse, inverse


def layer_norm_back(grad, normed, inverse):
    grad_mean = jnp.mean(grad, axis=-1, keepdims=True)
    proj = jnp.mean(grad * normed, axis=-1, keepdims=True)
    return inverse * (grad - grad_mean - normed * proj)


def gelu(vals):
    inner = GELU_C * (vals + GELU_A * (vals * vals * vals))
    return vals * (0.5 * (1.0 + jnp.tanh(inner)))


def gelu_and_slope(vals):
    square = vals * vals
    tanh_in = jnp.tanh(GELU_C * (vals + GELU_A * (square * vals)))
    cdf = 0.5 * (1.0 + tanh_in)
    slope = cdf + 0.5 * vals * (1.0 - tanh_in * tanh_in) * (GELU_C * (1.0 + (3.0 * GELU_A) * square))
    return vals * cdf, slope


def dot_plain(lhs, rhs):
    return jnp.dot(lhs, rhs, preferred_element_type=jnp.float32)


def dot_rows(lhs, rhs):
    return lax.dot_general(lhs, rhs, (((0,), (0,)), ((), ())), preferred_element_type=jnp.float32)


def dot_cols(lhs, rhs):
    return lax.dot_general(lhs, rhs, (((1,), (1,)), ((), ())), preferred_element_type=jnp.float32)


def two_copies(k, ups, downs, other, sem, to_chunk):
    layer = 2 - k // OCT
    part = pl.ds(pl.multiple_of((k % 4) * WIDE, WIDE), WIDE)
    for array, cond, spot in ((downs, (k % OCT) < 4, (layer, part)), (ups, (k % OCT) >= 4, (layer, slice(None), part))):
        @pl.when(cond)
        def _(array=array, spot=spot):
            pair = (array.at[spot], other)
            pltpu.make_async_copy(*(pair if to_chunk else pair[::-1]), sem).start()


def small_pieces(k, arrays):
    up_one, down_one, merge, head = arrays[0], arrays[1], arrays[2], arrays[5]
    if k == UP_ONE:
        return [(up_one.at[layer], (pl.ds(layer * THIN, THIN),)) for layer in range(4)]
    if k == DOWN_ONE:
        return [(down_one.at[layer], (pl.ds(0, WIDE), pl.ds(layer * THIN, THIN))) for layer in range(4)]
    if k == MERGE:
        return [(merge, (pl.ds(0, WIDE),))]
    if k == HEAD_A:
        return [(head.at[pl.ds(0, WIDE)], (pl.ds(0, WIDE),))]
    return [(head.at[pl.ds(WIDE, HEAD_REST)], (pl.ds(0, HEAD_REST),))]


def small_copies(k, arrays, other, sem, to_chunk):
    for piece, inside in small_pieces(k, arrays):
        pair = (piece, other.at[inside])
        pltpu.make_async_copy(*(pair if to_chunk else pair[::-1]), sem).start()


def wait_bytes(ref, sem):
    pltpu.make_async_copy(ref, ref, sem).wait()


def small_ref(k, ref):
    return ref.at[pl.ds(0, HEAD_REST)] if k == HEAD_B else ref


SMALL_ORDER = (UP_ONE, DOWN_ONE, MERGE, HEAD_A, HEAD_B)


def two_item(num):
    return (2 - num // OCT) * OCT + (num + 4) % OCT


def one_forward(num, resid_in, resid_out, cast):
    layer = num // 4
    rows = pl.ds(pl.multiple_of((num % 4) * PAD_ROWS, STEP), PAD_ROWS)
    lanes = pl.ds(pl.multiple_of(layer * THIN, THIN), THIN)
    resid = resid_in[rows, :].astype(jnp.float32)
    normed = layer_norm(resid).astype(jnp.bfloat16)
    act = gelu(dot_plain(normed, cast[UP_ONE, lanes, :])).astype(jnp.bfloat16)
    out = dot_plain(act, cast[DOWN_ONE, :, lanes])
    resid_out[rows, :] = (resid + out).astype(jnp.bfloat16)


def merge_forward(resid_one, cast, resid_two):
    value = jnp.zeros((PAD_ROWS, WIDE), jnp.float32)
    for part in range(4):
        value = value + dot_plain(resid_one[part * PAD_ROWS:(part + 1) * PAD_ROWS, :], cast[MERGE, part * THIN:(part + 1) * THIN, :])
    resid_two[...] = value.astype(jnp.bfloat16)


def pool_images(resid_two):
    pooled = [jnp.sum(resid_two[img * PAD_IMG:(img + 1) * PAD_IMG, :].astype(jnp.float32), axis=0, keepdims=True) / float(TOKENS_TWO) for img in range(2)]
    return jnp.concatenate(pooled + [jnp.zeros((14, WIDE), jnp.float32)], axis=0)


def grad_kernel(*refs):
    w_in, images, labels = refs[0:6], refs[6], refs[7]
    grads, resid_saved, grad_one, cast_one = refs[OCT:12]
    load_sem, store_sem, ring_w, out_ring, cast, resid_two, normed_two, act_two, slope_two, grad_two, total = refs[12:]

    def start_small(num):
        small_copies(SMALL_ORDER[num], w_in, ring_w.at[num], load_sem.at[SMALL_ORDER[num]], True)

    def start_two(num):
        k = two_item(num)
        two_copies(k, w_in[3], w_in[4], ring_w.at[(num + 5) % RING], load_sem.at[k], True)

    def cast_slot(k, slot):
        def step(num, carry):
            rows = pl.ds(pl.multiple_of(num * QUARTER, QUARTER), QUARTER)
            cast[k, rows, :] = ring_w[slot, rows, :].astype(jnp.bfloat16)
            return carry
        lax.fori_loop(0, OCT, step, 0)

    def cast_small(num):
        k = SMALL_ORDER[num]
        wait_bytes(small_ref(k, ring_w.at[num]), load_sem.at[k])
        cast_slot(k, num)
        if k == HEAD_B:
            cast[k, HEAD_REST:WIDE, :] = jnp.zeros((WIDE - HEAD_REST, WIDE), jnp.bfloat16)

    def cast_two(num):
        k = two_item(num)
        slot = (num + 5) % RING
        wait_bytes(ring_w.at[slot], load_sem.at[k])
        cast_slot(k, slot)
        @pl.when(num + RING < TWO_CHUNKS)
        def _():
            start_two(num + RING)

    for num in range(5):
        start_small(num)
    for num in range(3):
        start_two(num)
    for num in range(5):
        cast_small(num)
        start_two(num + 3)
    cast_one[0] = cast[DOWN_ONE]
    cast_one[1] = cast[UP_ONE]
    resid_saved[0] = images[...]

    def first(num, carry):
        layer = num // 4
        one_forward(num, resid_saved.at[layer], resid_saved.at[layer + 1], cast)
        cast_two(num)
        return carry

    lax.fori_loop(0, PAIR, first, 0)
    merge_forward(resid_saved.at[4], cast, resid_two.at[0])

    def second(num, carry):
        layer, part = num // 4, num % 4
        lanes = pl.ds(pl.multiple_of(part * WIDE, WIDE), WIDE)
        @pl.when(part == 0)
        def _():
            normed_two[layer] = layer_norm(resid_two[layer].astype(jnp.float32)).astype(jnp.bfloat16)
            total[...] = jnp.zeros_like(total)
        @pl.when(num < OCT)
        def _():
            cast_two(num + PAIR)
        pre = dot_plain(normed_two[layer], cast[(2 - layer) * OCT + 4 + part])
        act, slope = gelu_and_slope(pre)
        act = act.astype(jnp.bfloat16)
        act_two[layer, :, lanes] = act
        slope_two[layer, :, lanes] = slope
        total[...] += dot_plain(act, cast[(2 - layer) * OCT + part])
        @pl.when(part == 3)
        def _():
            resid_two[layer + 1] = (resid_two[layer].astype(jnp.float32) + total[...]).astype(jnp.bfloat16)
        return carry

    lax.fori_loop(0, 12, second, 0)

    pooled = pool_images(resid_two.at[3])
    head_norm, head_inv = layer_norm_parts(pooled)
    head_in = head_norm.astype(jnp.bfloat16)
    logits = jnp.concatenate([dot_cols(head_in, cast[HEAD_A]), dot_cols(head_in, cast[HEAD_B])], axis=1)
    ids = lax.broadcasted_iota(jnp.int32, (PAIR, 1024), 1)
    row = lax.broadcasted_iota(jnp.int32, (PAIR, 1024), 0)
    logits = jnp.where(ids < CLASSES, logits, -jnp.inf)
    expo = jnp.exp(logits - jnp.max(logits, axis=1, keepdims=True))
    probs = expo / jnp.sum(expo, axis=1, keepdims=True)
    target = jnp.where(row == 0, labels[0], labels[1])
    onehot = (ids == target).astype(jnp.float32)
    grad_logits = jnp.where(row < 2, (probs - onehot) / 64.0, 0.0).astype(jnp.bfloat16)

    def out_chunk(k, slot, fresh, value):
        @pl.when(jnp.logical_not(fresh))
        def _():
            wait_bytes(out_ring.at[slot], store_sem.at[slot])
        out_ring[slot] = value.astype(jnp.bfloat16)
        pltpu.make_async_copy(out_ring.at[slot], grads.at[k], store_sem.at[slot]).start()

    true = jnp.bool_(True)
    out_chunk(HEAD_A, 0, true, dot_rows(grad_logits[:, 0:WIDE], head_in))
    out_chunk(HEAD_B, 1, true, dot_rows(grad_logits[:, WIDE:1024], head_in))
    grad_head = dot_plain(grad_logits[:, 0:WIDE], cast[HEAD_A]) + dot_plain(grad_logits[:, WIDE:1024], cast[HEAD_B])
    grad_pooled = (layer_norm_back(grad_head, head_norm, head_inv) / float(TOKENS_TWO)).astype(jnp.bfloat16).astype(jnp.float32)
    spot = lax.broadcasted_iota(jnp.int32, (PAD_IMG, WIDE), 0)
    for img in range(2):
        spread = jnp.where(spot < TOKENS_TWO, jnp.broadcast_to(grad_pooled[img:img + 1], (PAD_IMG, WIDE)), 0.0)
        grad_two[img * PAD_IMG:(img + 1) * PAD_IMG, :] = spread.astype(jnp.bfloat16)

    def third(num, carry):
        layer, part = 2 - num // 4, num % 4
        lanes = pl.ds(pl.multiple_of(part * WIDE, WIDE), WIDE)
        base = (num // 4) * OCT + part
        slot = (num * 2 + 2) % RING
        fresh = num < 3
        @pl.when(part == 0)
        def _():
            total[...] = jnp.zeros_like(total)
        out_chunk(base, slot, fresh, dot_rows(act_two[layer, :, lanes], grad_two[...]))
        grad_act = dot_cols(grad_two[...], cast[base])
        grad_pre = (grad_act * slope_two[layer, :, lanes]).astype(jnp.bfloat16)
        out_chunk(base + 4, slot + 1, fresh, dot_rows(normed_two[layer], grad_pre))
        total[...] += dot_cols(grad_pre, cast[base + 4])
        @pl.when(part == 3)
        def _():
            normed, inverse = layer_norm_parts(resid_two[layer].astype(jnp.float32))
            grad_in = layer_norm_back(total[...], normed, inverse) + grad_two[...].astype(jnp.float32)
            grad_two[...] = grad_in.astype(jnp.bfloat16)
        return carry

    lax.fori_loop(0, 12, third, 0)
    wait_bytes(out_ring.at[2], store_sem.at[2])
    for part in range(4):
        rows = slice(part * PAD_ROWS, (part + 1) * PAD_ROWS)
        spots = slice(part * THIN, (part + 1) * THIN)
        out_ring[2, spots, :] = dot_rows(resid_saved[4, rows, :], grad_two[...]).astype(jnp.bfloat16)
        grad_one[rows, :] = dot_cols(grad_two[...], cast[MERGE, spots, :]).astype(jnp.bfloat16)
    pltpu.make_async_copy(out_ring.at[2], grads.at[MERGE], store_sem.at[2]).start()
    for slot in range(RING):
        wait_bytes(out_ring.at[slot], store_sem.at[slot])


def forward_and_grads(params, images, labels):
    any_hbm = pl.BlockSpec(memory_space=pltpu.HBM)
    in_vmem = pl.BlockSpec(memory_space=pltpu.VMEM)
    return pl.pallas_call(
        grad_kernel,
        out_shape=[
            jax.ShapeDtypeStruct((27, WIDE, WIDE), jnp.bfloat16),
            jax.ShapeDtypeStruct((5, 4 * PAD_ROWS, THIN), jnp.bfloat16),
            jax.ShapeDtypeStruct((4 * PAD_ROWS, THIN), jnp.bfloat16),
            jax.ShapeDtypeStruct((2, WIDE, WIDE), jnp.bfloat16),
        ],
        in_specs=[any_hbm] * 6 + [in_vmem, pl.BlockSpec(memory_space=pltpu.SMEM)],
        out_specs=[any_hbm] + [in_vmem] * 3,
        scratch_shapes=[
            pltpu.SemaphoreType.DMA((CHUNKS,)),
            pltpu.SemaphoreType.DMA((RING,)),
            pltpu.VMEM((RING, WIDE, WIDE), jnp.float32),
            pltpu.VMEM((RING, WIDE, WIDE), jnp.bfloat16),
            pltpu.VMEM((CHUNKS, WIDE, WIDE), jnp.bfloat16),
            pltpu.VMEM((4, PAD_ROWS, WIDE), jnp.bfloat16),
            pltpu.VMEM((3, PAD_ROWS, WIDE), jnp.bfloat16),
            pltpu.VMEM((3, PAD_ROWS, 2048), jnp.bfloat16),
            pltpu.VMEM((3, PAD_ROWS, 2048), jnp.float32),
            pltpu.VMEM((PAD_ROWS, WIDE), jnp.bfloat16),
            pltpu.VMEM((PAD_ROWS, WIDE), jnp.float32),
        ],
        compiler_params=pltpu.CompilerParams(vmem_limit_bytes=62 * 2**20),
        cost_estimate=pl.CostEstimate(flops=3 * 10**10, bytes_accessed=5 * 10**7, transcendentals=0),
    )(*params, images, labels)


def block_squares(read, sums, chunk):
    def step(num, carry):
        total = jnp.zeros((OCT, LANES), jnp.float32)
        for part in range(4):
            vals = read(pl.ds(pl.multiple_of(num * THIN + part * STEP, STEP), STEP)).astype(jnp.float32)
            vals = vals * vals
            total = total + (vals[0:OCT] + vals[OCT:PAIR]) + (vals[PAIR:TWO_CHUNKS] + vals[TWO_CHUNKS:STEP])
        sums[chunk, pl.ds(num, 1), :] = jnp.sum(total, axis=0, keepdims=True)
        return carry
    lax.fori_loop(0, 4, step, 0)


TILE = 208
TILES = OCT


def reduce_kernel(*refs):
    grads, w_in = refs[0], refs[1:7]
    resid_saved, grad_in, cast_one = refs[7:10]
    out, w_sums, g_sums = refs[10:13]
    load_sem, out_sem, w_sem, w_buf, grad_one, up_total, down_total = refs[13:20]
    bufs = refs[20:]
    grad_buf, full_buf = bufs[0:2]

    def load(k, carry):
        pltpu.make_async_copy(grads.at[k], grad_buf.at[k], load_sem.at[k]).start()
        return carry

    lax.fori_loop(0, 27, load, 0)

    def w_start(k):
        two_copies(k, w_in[3], w_in[4], w_buf.at[k % W_RING], w_sem.at[k], True)

    def w_sum(k):
        slot = k % W_RING
        block_squares(lambda rows: w_buf[slot, rows, :], w_sums, k)

    for k in range(W_RING):
        w_start(jnp.int32(k))
    grad_one[...] = grad_in[...]

    def one_backward(num, carry):
        layer, tile = 3 - num // TILES, num % TILES
        rows = pl.ds(pl.multiple_of(tile * TILE, PAIR), TILE)
        lanes = pl.ds(pl.multiple_of(layer * THIN, THIN), THIN)
        normed, inverse = layer_norm_parts(resid_saved[layer, rows, :].astype(jnp.float32))
        normed_b = normed.astype(jnp.bfloat16)
        up = cast_one[1, lanes, :]
        act, slope = gelu_and_slope(dot_plain(normed_b, up))
        grad = grad_one[rows, :]
        keep = jnp.where(tile == 0, 0.0, 1.0)
        down_total[...] = down_total[...] * keep + dot_rows(act.astype(jnp.bfloat16), grad)
        grad_pre = (dot_cols(grad, cast_one[0, :, lanes]) * slope).astype(jnp.bfloat16)
        up_total[...] = up_total[...] * keep + dot_rows(normed_b, grad_pre)
        back = layer_norm_back(dot_cols(grad_pre, up), normed, inverse) + grad.astype(jnp.float32)
        grad_one[rows, :] = back.astype(jnp.bfloat16)
        @pl.when(tile == TILES - 1)
        def _():
            grad_buf[DOWN_ONE, :, lanes] = down_total[...].astype(jnp.bfloat16)
            grad_buf[UP_ONE, lanes, :] = up_total[...].astype(jnp.bfloat16)
        return carry

    down_total[...] = jnp.zeros_like(down_total)
    up_total[...] = jnp.zeros_like(up_total)

    def each_tick(t):
        @pl.when(t < PAIR)
        def _():
            lax.fori_loop(t * 2, t * 2 + 2, one_backward, 0)

        @pl.when(t < TWO_CHUNKS)
        def _():
            wait_bytes(w_buf.at[t % W_RING], w_sem.at[t])
            w_sum(t)

        @pl.when(t + W_RING < TWO_CHUNKS)
        def _():
            w_start(t + W_RING)

        for k in range(TWO_CHUNKS, CHUNKS):
            @pl.when(t == k - W_RING)
            def _(k=k):
                small_copies(k, w_in, w_buf.at[k % W_RING], w_sem.at[k], True)

            @pl.when(t == k)
            def _(k=k):
                wait_bytes(small_ref(k, w_buf.at[k % W_RING]), w_sem.at[k])
                if k == HEAD_B:
                    w_buf[k % W_RING, HEAD_REST:WIDE, :] = jnp.zeros((WIDE - HEAD_REST, WIDE), jnp.float32)
                w_sum(k)

    def before(k):
        @pl.when(k < 27)
        def _():
            wait_bytes(grad_buf.at[k], load_sem.at[k])

    def after(k):
        pltpu.make_async_copy(full_buf.at[k], out.at[k], out_sem.at[k]).start()
        block_squares(lambda rows: full_buf[k, rows, :], g_sums, k)

    all_reduce_body(CHUNKS, *bufs, before, after, each_tick)

    def finish(k, carry):
        wait_bytes(full_buf.at[k], out_sem.at[k])
        return carry

    lax.fori_loop(0, CHUNKS, finish, 0)


def reduce_grads(grads, params, resid_saved, grad_one, cast_one):
    any_hbm = pl.BlockSpec(memory_space=pltpu.HBM)
    in_vmem = pl.BlockSpec(memory_space=pltpu.VMEM)
    sums_shape = (CHUNKS, 4, LANES)
    return pl.pallas_call(
        reduce_kernel,
        out_shape=[jax.ShapeDtypeStruct((CHUNKS, WIDE, WIDE), jnp.bfloat16)] + [jax.ShapeDtypeStruct(sums_shape, jnp.float32)] * 2,
        in_specs=[any_hbm] * 7 + [in_vmem] * 3,
        out_specs=[any_hbm] + [in_vmem] * 2,
        scratch_shapes=[pltpu.SemaphoreType.DMA((CHUNKS,))] * 3 + [
            pltpu.VMEM((W_RING, WIDE, WIDE), jnp.float32),
            pltpu.VMEM((4 * PAD_ROWS, THIN), jnp.bfloat16),
            pltpu.VMEM((THIN, WIDE), jnp.float32),
            pltpu.VMEM((WIDE, THIN), jnp.float32),
        ] + scratch(CHUNKS, WIDE),
        compiler_params=pltpu.CompilerParams(has_side_effects=True, vmem_limit_bytes=62 * 2**20),
        cost_estimate=pl.CostEstimate(flops=10**10, bytes_accessed=6 * 10**7, transcendentals=0),
    )(grads, *params, resid_saved, grad_one, cast_one)


def next_kernel(*refs):
    grads, w_in, v_in = refs[0], refs[1:7], refs[7:13]
    w_sums, g_sums, images = refs[13:PAIR]
    logits, w_out, v_out = refs[PAIR], refs[17:23], refs[23:29]
    load_sem, store_sem, ring_w, ring_v, ring_g, cast, coef, resid_one, resid_two, normed_two, total_two = refs[29:]
    rings = (ring_w, ring_v)

    def start_small(num):
        k = SMALL_ORDER[num]
        for which, arrays in enumerate((w_in, v_in)):
            small_copies(k, arrays, rings[which].at[num], load_sem.at[which, k], True)
        pltpu.make_async_copy(grads.at[k], ring_g.at[num], load_sem.at[2, k]).start()

    def start_two(num):
        k = two_item(num)
        slot = (num + 5) % RING
        for which, arrays in enumerate((w_in, v_in)):
            two_copies(k, arrays[3], arrays[4], rings[which].at[slot], load_sem.at[which, k], True)
        pltpu.make_async_copy(grads.at[k], ring_g.at[slot], load_sem.at[2, k]).start()

    for num in range(5):
        start_small(num)

    def ratio(w_total, g_total):
        return TRUST * (jnp.sqrt(w_total) / jnp.sqrt(g_total))

    def total(sums, first, size):
        return jnp.sum(jnp.sum(jnp.sum(sums[first:first + size], axis=0), axis=0, keepdims=True), axis=1, keepdims=True)

    for first, size in [(0, 4), (4, 4), (OCT, 4), (12, 4), (PAIR, 4), (20, 4), (HEAD_A, 2), (MERGE, 1)]:
        value = ratio(total(w_sums, first, size), total(g_sums, first, size))
        for k in range(first, first + size):
            coef[k] = jnp.broadcast_to(value, (4, LANES))
    by_row = ratio(jnp.sum(w_sums[UP_ONE], axis=1, keepdims=True), jnp.sum(g_sums[UP_ONE], axis=1, keepdims=True))
    coef[UP_ONE] = jnp.broadcast_to(by_row, (4, LANES))
    for layer in range(4):
        lanes = pl.ds(layer * THIN, THIN)
        lane_total = [jnp.sum(jnp.sum(sums[DOWN_ONE, :, lanes], axis=0, keepdims=True), axis=1, keepdims=True) for sums in (w_sums, g_sums)]
        coef[DOWN_ONE, :, lanes] = jnp.broadcast_to(ratio(*lane_total), (4, THIN))

    def apply_update(k, slot):
        def step(num, carry):
            rows = pl.ds(pl.multiple_of(num * STEP, STEP), STEP)
            factor = coef[k, pl.ds(num // 4, 1), :]
            new_v = MOMENTUM * ring_v[slot, rows, :] + factor * ring_g[slot, rows, :].astype(jnp.float32)
            new_w = ring_w[slot, rows, :] - new_v
            ring_v[slot, rows, :] = new_v
            ring_w[slot, rows, :] = new_w
            cast[k, rows, :] = new_w.astype(jnp.bfloat16)
            return carry
        lax.fori_loop(0, PAIR, step, 0)

    def update_small(num):
        k = SMALL_ORDER[num]
        for which in range(2):
            wait_bytes(small_ref(k, rings[which].at[num]), load_sem.at[which, k])
        wait_bytes(ring_g.at[num], load_sem.at[2, k])
        apply_update(k, num)
        if k == HEAD_B:
            cast[k, HEAD_REST:WIDE, :] = jnp.zeros((WIDE - HEAD_REST, WIDE), jnp.bfloat16)
        for which, arrays in enumerate((w_out, v_out)):
            small_copies(k, arrays, rings[which].at[num], store_sem.at[which, k], False)

    def wait_small_store(num):
        k = SMALL_ORDER[num]
        for which in range(2):
            wait_bytes(small_ref(k, rings[which].at[num]), store_sem.at[which, k])

    def wait_two_store(num):
        k = two_item(num)
        slot = (num + 5) % RING
        for which in range(2):
            wait_bytes(rings[which].at[slot], store_sem.at[which, k])

    def update_two(num, carry):
        k = two_item(num)
        slot = (num + 5) % RING
        for which in range(2):
            wait_bytes(rings[which].at[slot], load_sem.at[which, k])
        wait_bytes(ring_g.at[slot], load_sem.at[2, k])
        apply_update(k, slot)
        for which, arrays in enumerate((w_out, v_out)):
            two_copies(k, arrays[3], arrays[4], rings[which].at[slot], store_sem.at[which, k], False)
        later = num + AHEAD
        @pl.when((later < TWO_CHUNKS) & (later >= RING))
        def _():
            wait_two_store(later - RING)
        @pl.when(later < TWO_CHUNKS)
        def _():
            start_two(later)
        return carry

    for num in range(3):
        start_two(num)
    for num in range(5):
        update_small(num)
    resid_one[...] = images[...]
    wait_small_store(0)
    start_two(3)

    def first(num, carry):
        for small in range(1, 5):
            @pl.when(num == small - 1)
            def _(small=small):
                wait_small_store(small)
        update_two(num, 0)

        def body(part, carry):
            one_forward(part, resid_one, resid_one, cast)
            return carry

        return lax.fori_loop(num * 2, num * 2 + 2, body, carry)

    lax.fori_loop(0, OCT, first, 0)
    merge_forward(resid_one, cast, resid_two)

    def second(num, carry):
        layer, part = num // 4, num % 4
        @pl.when(part == 0)
        def _():
            normed_two[...] = layer_norm(resid_two[...].astype(jnp.float32)).astype(jnp.bfloat16)
            total_two[...] = jnp.zeros_like(total_two)
        @pl.when(layer < 2)
        def _():
            lax.fori_loop(OCT + num * 2, 10 + num * 2, update_two, 0)
        act = gelu(dot_plain(normed_two[...], cast[(2 - layer) * OCT + 4 + part])).astype(jnp.bfloat16)
        total_two[...] += dot_plain(act, cast[(2 - layer) * OCT + part])
        @pl.when(part == 3)
        def _():
            resid_two[...] = (resid_two[...].astype(jnp.float32) + total_two[...]).astype(jnp.bfloat16)
        return carry

    lax.fori_loop(0, 12, second, 0)
    head_in = layer_norm(pool_images(resid_two)).astype(jnp.bfloat16)
    logits[:, 0:WIDE] = dot_cols(head_in, cast[HEAD_A])[0:2]
    logits[:, WIDE:1000] = dot_cols(head_in, cast[HEAD_B])[0:2, 0:HEAD_REST]
    for num in range(PAIR, TWO_CHUNKS):
        wait_two_store(num)


def arrange(images):
    count, tokens, width = images.shape
    split = images.reshape(count, tokens // 4, 4, width).transpose(2, 0, 1, 3)
    split = jnp.pad(split, ((0, 0), (0, 0), (0, PAD_IMG - tokens // 4), (0, 0)))
    return split.reshape(4 * count * PAD_IMG, width)


def update_and_forward(params, velocities, grads, w_sums, g_sums, images):
    any_hbm = pl.BlockSpec(memory_space=pltpu.HBM)
    in_vmem = pl.BlockSpec(memory_space=pltpu.VMEM)
    shapes = [jax.ShapeDtypeStruct(array.shape, array.dtype) for array in params]
    outs = pl.pallas_call(
        next_kernel,
        out_shape=[jax.ShapeDtypeStruct((2, CLASSES), jnp.float32)] + shapes + shapes,
        in_specs=[any_hbm] * 13 + [in_vmem] * 3,
        out_specs=[in_vmem] + [any_hbm] * 12,
        scratch_shapes=[
            pltpu.SemaphoreType.DMA((3, CHUNKS)),
            pltpu.SemaphoreType.DMA((2, CHUNKS)),
            pltpu.VMEM((RING, WIDE, WIDE), jnp.float32),
            pltpu.VMEM((RING, WIDE, WIDE), jnp.float32),
            pltpu.VMEM((RING, WIDE, WIDE), jnp.bfloat16),
            pltpu.VMEM((CHUNKS, WIDE, WIDE), jnp.bfloat16),
            pltpu.VMEM((CHUNKS, 4, LANES), jnp.float32),
            pltpu.VMEM((4 * PAD_ROWS, THIN), jnp.bfloat16),
            pltpu.VMEM((PAD_ROWS, WIDE), jnp.bfloat16),
            pltpu.VMEM((PAD_ROWS, WIDE), jnp.bfloat16),
            pltpu.VMEM((PAD_ROWS, WIDE), jnp.float32),
        ],
        compiler_params=pltpu.CompilerParams(vmem_limit_bytes=58 * 2**20),
        cost_estimate=pl.CostEstimate(flops=10**10, bytes_accessed=135 * 10**6, transcendentals=0),
    )(grads, *params, *velocities, w_sums, g_sums, images)
    return outs


def solution(mesh):
    def local_step(x_now, labels_now, x_next, *weights):
        params = weights[0:5] + (weights[5].T,)
        velocities = weights[6:11] + (weights[11].T,)
        grads, resid_saved, grad_one, cast_one = forward_and_grads(params, arrange(x_now), labels_now)
        sums, w_sums, g_sums = reduce_grads(grads, params, resid_saved, grad_one, cast_one)
        outs = update_and_forward(params, velocities, sums, w_sums, g_sums, arrange(x_next))
        new_w, new_v = outs[1:7], outs[7:13]
        return (outs[0],) + tuple(new_w[0:5]) + (new_w[5].T,) + tuple(new_v[0:5]) + (new_v[5].T,)

    replicated = P()
    batch_split = P('data')
    in_specs = (batch_split, batch_split, batch_split) + (replicated,) * 12
    out_specs = (batch_split,) + (replicated,) * 12
    return jax.shard_map(local_step, mesh=mesh, in_specs=in_specs, out_specs=out_specs, check_vma=False)
```

time: 405 us -> 265 us (0.65); the launches traced: 398 us -> 265 us
  Pallas kernels: 128 us -> 261 us
  other arithmetic: 120 us -> 0 us
  matrix products: 116 us -> 0 us
  local copies, waits for them, and re-layouts: 27.7 us -> 3.7 us
  between operations: 5.43 us -> 0.67 us
    pallas_call x1 -> x3, Pallas kernels: 128 us -> 261 us  [the longest x1 147 us: reduce_grads(): pl.pallas_call(reduce_kernel, out_shape=[jax.ShapeDtypeStruct((CHUNKS, WI...]
    dot_general x55 -> x0, matrix products: 116 us -> none  [the longest x14 39.3 us: block_forward(): block_out = jnp.dot(activated_b, w_down, preferred_element_type=jnp.float32)]
    reduce_sum x42 -> x0, other arithmetic: 57.6 us -> none  [the longest x6 30.1 us: lars_step(): w_norm = jnp.sqrt(jnp.sum(weight * weight, axis=red_axes, keepdims=True))]
    another operation x4 -> x0, other arithmetic: 47.4 us -> none
    unnamed x216 -> x0, local copies, waits for them, and re-layouts: 23 us -> none
    sub x2 -> x0, other arithmetic: 7.38 us -> none  [lars_step(): return (weight - new_vel, new_vel)]
    convert_element_type x10 -> x0, other arithmetic: 6.89 us -> none  [the longest x3 4.68 us: block_forward(): normed_b = normed.astype(jnp.bfloat16)]
where the time goes in v2:
time: 265 us
  Pallas kernels  261 us (98%)
  local copies, waits for them, and re-layouts  3.7 us (1%)
    pallas_call x1, Pallas kernels, reduce_grads(): pl.pallas_call(reduce_kernel, out_shape=[jax.ShapeDtypeStruct((CHUNKS, WI...  147 us
    pallas_call x1, Pallas kernels, forward_and_grads(): pl.pallas_call(grad_kernel, out_shape=[jax.ShapeDtypeStruct((27, WIDE, WI...  59.4 us
    pallas_call x1, Pallas kernels, update_and_forward(): pl.pallas_call(next_kernel, out_shape=[jax.ShapeDtypeStruct((2, CLASSES),...  54.7 us

profile of v2, /device:TPU:0, one launch (start us, length us, event | category | flops | bytes accessed | tf_op | source)
XLA Modules:
  0.0 265.2 jit_solution(11407347362967411603)
XLA Ops:
  0.6 1.1 copy.33
  1.7 0.8 pad.7
  2.5 1.1 copy.32
  3.6 0.8 pad.8
  4.4 59.4 %shard_map.246 = (bf16[27,512,512]{2,1,0:T(8,128)(2,1)}, bf16[5,1664,128]{2,1,0:T(8,128)(2,1)}, bf16[1664,128]{1,0:T(8,128)(2,1)}, bf16[2,512,512]{2,1,0:T(8,128)(2,1)}) custom-call(f32[4,128,512]{2,1,0:T(8,128)} %refs_1_.5, f32[4,512,128]{2,1,0:T(8,128)} %refs_2_.5, f32[512,512]{1,0:T(8,128)} %refs_3_.5, f32[3,512,2048]{2,1,0:T(8,128)} %refs_4_.5, ...), custom_call_target="tpu_custom_call" | custom-call | flops 30000001024 | bytes 50000000 | tf_op jit(solution)/shard_map/pallas_call | solution.py:489
  63.8 146.7 %shard_map.247 = (bf16[29,512,512]{2,1,0:T(8,128)(2,1)}, f32[29,4,512]{2,1,0:T(4,128)}, f32[29,4,512]{2,1,0:T(4,128)}) custom-call(bf16[27,512,512]{2,1,0:T(8,128)(2,1)} %get-tuple-element.33.refs_0_, f32[4,128,512]{2,1,0:T(8,128)} %refs_1_.5, f32[4,512,128]{2,1,0:T(8,128)} %refs_2_.5, f32[512,512]{1,0:T(8,128)} %refs_3_.5, f32[3,512,2048]{2,1,0:T(8,128)} %refs_4_.5, ...), custom_call_target="tpu_custom_call" | custom-call | flops 10000000000 | bytes 60000000 | tf_op jit(solution)/shard_map/pallas_call | solution.py:630
  210.5 54.7 %shard_map.248 = (f32[2,1000]{1,0:T(2,128)}, f32[4,128,512]{2,1,0:T(8,128)}, f32[4,512,128]{2,1,0:T(8,128)}, f32[512,512]{1,0:T(8,128)}, f32[3,512,2048]{2,1,0:T...) custom-call(bf16[29,512,512]{2,1,0:T(8,128)(2,1)} %get-tuple-element, ...), custom_call_target="tpu_custom_call" | custom-call | flops 10000000000 | bytes 135000000 | tf_op jit(solution)/shard_map/pallas_call | solution.py:797

commit v3 on v2

--- a/solution.py
+++ b/solution.py
@@ -19,6 +19,7 @@
 AHEAD = 4
 W_RING = 3
 TOKENS_TWO = 196
+TOKENS = 784
 PAD_IMG = 208
 PAD_ROWS = 416
 GELU_C = 0.7978845608028654
@@ -31,11 +32,12 @@
 TWO_CHUNKS = 24
 OCT = 8
 PAIR = 16
+DOZEN = 12
 
 MESH = pl.DeviceIdType.MESH
 ROWS = WIDE
 LAG = 3
-STAGES = 12
+STAGES = DOZEN
 
 
 def all_reduce_body(chunks, grad_buf, full_buf, recv_core, recv_one, recv_z, recv_mid, recv_two, send_sem, recv_sem, before, after, extra):
@@ -206,10 +208,11 @@
     stages = (stage_0, stage_1, stage_2, stage_3, stage_4, stage_5, stage_6, stage_7, stage_8, stage_9, stage_10, stage_11, stage_12)
 
     def tick(t, carry):
-        for num, stage in enumerate(stages):
+        for num, stage in reversed(list(enumerate(stages))):
+            if num == 0:
+                extra(t)
             k = t - num * LAG
             pl.when((k >= 0) & (k < chunks))(functools.partial(stage, k))
-        extra(t)
         return carry
 
     lax.fori_loop(0, chunks + STAGES * LAG, tick, 0)
@@ -342,10 +345,24 @@
     return jnp.concatenate(pooled + [jnp.zeros((14, WIDE), jnp.float32)], axis=0)
 
 
+def arrange(images, wide, resid):
+    for img in range(2):
+        wide[img * TOKENS:(img + 1) * TOKENS, :] = images[img].astype(jnp.float32)
+    resid[...] = jnp.zeros_like(resid)
+    for part in range(4):
+        for img in range(2):
+            first = part * PAD_ROWS + img * PAD_IMG
+            rows = wide[pl.ds(img * TOKENS + part, TOKENS_TWO, stride=4), :]
+            resid[first:first + TOKENS_TWO, :] = rows.astype(jnp.bfloat16)
+
+
 def grad_kernel(*refs):
     w_in, images, labels = refs[0:6], refs[6], refs[7]
-    grads, resid_saved, grad_one, cast_one = refs[OCT:12]
-    load_sem, store_sem, ring_w, out_ring, cast, resid_two, normed_two, act_two, slope_two, grad_two, total = refs[12:]
+    head_grads, cast_out, act_out, slope_out, resid_saved, resid_two, grad_two, cast_one = refs[OCT:PAIR]
+    load_sem, cast_sem, act_sem, slope_sem, ring_w, cast, last_two, normed_two, act_two, slope_two, total, wide = refs[PAIR:]
+
+    def send_cast(k, spot):
+        pltpu.make_async_copy(cast.at[k], cast_out.at[spot], cast_sem.at[spot]).start()
 
     def start_small(num):
         small_copies(SMALL_ORDER[num], w_in, ring_w.at[num], load_sem.at[SMALL_ORDER[num]], True)
@@ -373,6 +390,7 @@
         slot = (num + 5) % RING
         wait_bytes(ring_w.at[slot], load_sem.at[k])
         cast_slot(k, slot)
+        send_cast(k, k)
         @pl.when(num + RING < TWO_CHUNKS)
         def _():
             start_two(num + RING)
@@ -384,9 +402,10 @@
     for num in range(5):
         cast_small(num)
         start_two(num + 3)
+    send_cast(MERGE, TWO_CHUNKS)
     cast_one[0] = cast[DOWN_ONE]
     cast_one[1] = cast[UP_ONE]
-    resid_saved[0] = images[...]
+    arrange(images, wide, resid_saved.at[0])
 
     def first(num, carry):
         layer = num // 4
@@ -402,25 +421,33 @@
         lanes = pl.ds(pl.multiple_of(part * WIDE, WIDE), WIDE)
         @pl.when(part == 0)
         def _():
-            normed_two[layer] = layer_norm(resid_two[layer].astype(jnp.float32)).astype(jnp.bfloat16)
+            normed_two[...] = layer_norm(resid_two[layer].astype(jnp.float32)).astype(jnp.bfloat16)
             total[...] = jnp.zeros_like(total)
         @pl.when(num < OCT)
         def _():
             cast_two(num + PAIR)
-        pre = dot_plain(normed_two[layer], cast[(2 - layer) * OCT + 4 + part])
+        pre = dot_plain(normed_two[...], cast[(2 - layer) * OCT + 4 + part])
         act, slope = gelu_and_slope(pre)
         act = act.astype(jnp.bfloat16)
         act_two[layer, :, lanes] = act
         slope_two[layer, :, lanes] = slope
         total[...] += dot_plain(act, cast[(2 - layer) * OCT + part])
+        pltpu.make_async_copy(act_two.at[layer, :, lanes], act_out.at[layer, :, lanes], act_sem.at[num]).start()
+        pltpu.make_async_copy(slope_two.at[layer, :, lanes], slope_out.at[layer, :, lanes], slope_sem.at[num]).start()
         @pl.when(part == 3)
         def _():
-            resid_two[layer + 1] = (resid_two[layer].astype(jnp.float32) + total[...]).astype(jnp.bfloat16)
-        return carry
-
-    lax.fori_loop(0, 12, second, 0)
-
-    pooled = pool_images(resid_two.at[3])
+            value = (resid_two[layer].astype(jnp.float32) + total[...]).astype(jnp.bfloat16)
+            @pl.when(layer < 2)
+            def _():
+                resid_two[jnp.minimum(layer + 1, 2)] = value
+            @pl.when(layer == 2)
+            def _():
+                last_two[...] = value
+        return carry
+
+    lax.fori_loop(0, DOZEN, second, 0)
+
+    pooled = pool_images(last_two)
     head_norm, head_inv = layer_norm_parts(pooled)
     head_in = head_norm.astype(jnp.bfloat16)
     logits = jnp.concatenate([dot_cols(head_in, cast[HEAD_A]), dot_cols(head_in, cast[HEAD_B])], axis=1)
@@ -433,16 +460,8 @@
     onehot = (ids == target).astype(jnp.float32)
     grad_logits = jnp.where(row < 2, (probs - onehot) / 64.0, 0.0).astype(jnp.bfloat16)
 
-    def out_chunk(k, slot, fresh, value):
-        @pl.when(jnp.logical_not(fresh))
-        def _():
-            wait_bytes(out_ring.at[slot], store_sem.at[slot])
-        out_ring[slot] = value.astype(jnp.bfloat16)
-        pltpu.make_async_copy(out_ring.at[slot], grads.at[k], store_sem.at[slot]).start()
-
-    true = jnp.bool_(True)
-    out_chunk(HEAD_A, 0, true, dot_rows(grad_logits[:, 0:WIDE], head_in))
-    out_chunk(HEAD_B, 1, true, dot_rows(grad_logits[:, WIDE:1024], head_in))
+    head_grads[0] = dot_rows(grad_logits[:, 0:WIDE], head_in).astype(jnp.bfloat16)
+    head_grads[1] = dot_rows(grad_logits[:, WIDE:1024], head_in).astype(jnp.bfloat16)
     grad_head = dot_plain(grad_logits[:, 0:WIDE], cast[HEAD_A]) + dot_plain(grad_logits[:, WIDE:1024], cast[HEAD_B])
     grad_pooled = (layer_norm_back(grad_head, head_norm, head_inv) / float(TOKENS_TWO)).astype(jnp.bfloat16).astype(jnp.float32)
     spot = lax.broadcasted_iota(jnp.int32, (PAD_IMG, WIDE), 0)
@@ -450,37 +469,19 @@
         spread = jnp.where(spot < TOKENS_TWO, jnp.broadcast_to(grad_pooled[img:img + 1], (PAD_IMG, WIDE)), 0.0)
         grad_two[img * PAD_IMG:(img + 1) * PAD_IMG, :] = spread.astype(jnp.bfloat16)
 
-    def third(num, carry):
-        layer, part = 2 - num // 4, num % 4
-        lanes = pl.ds(pl.multiple_of(part * WIDE, WIDE), WIDE)
-        base = (num // 4) * OCT + part
-        slot = (num * 2 + 2) % RING
-        fresh = num < 3
-        @pl.when(part == 0)
-        def _():
-            total[...] = jnp.zeros_like(total)
-        out_chunk(base, slot, fresh, dot_rows(act_two[layer, :, lanes], grad_two[...]))
-        grad_act = dot_cols(grad_two[...], cast[base])
-        grad_pre = (grad_act * slope_two[layer, :, lanes]).astype(jnp.bfloat16)
-        out_chunk(base + 4, slot + 1, fresh, dot_rows(normed_two[layer], grad_pre))
-        total[...] += dot_cols(grad_pre, cast[base + 4])
-        @pl.when(part == 3)
-        def _():
-            normed, inverse = layer_norm_parts(resid_two[layer].astype(jnp.float32))
-            grad_in = layer_norm_back(total[...], normed, inverse) + grad_two[...].astype(jnp.float32)
-            grad_two[...] = grad_in.astype(jnp.bfloat16)
-        return carry
-
-    lax.fori_loop(0, 12, third, 0)
-    wait_bytes(out_ring.at[2], store_sem.at[2])
-    for part in range(4):
-        rows = slice(part * PAD_ROWS, (part + 1) * PAD_ROWS)
-        spots = slice(part * THIN, (part + 1) * THIN)
-        out_ring[2, spots, :] = dot_rows(resid_saved[4, rows, :], grad_two[...]).astype(jnp.bfloat16)
-        grad_one[rows, :] = dot_cols(grad_two[...], cast[MERGE, spots, :]).astype(jnp.bfloat16)
-    pltpu.make_async_copy(out_ring.at[2], grads.at[MERGE], store_sem.at[2]).start()
-    for slot in range(RING):
-        wait_bytes(out_ring.at[slot], store_sem.at[slot])
+    def finish(num, carry):
+        lanes = pl.ds(pl.multiple_of((num % 4) * WIDE, WIDE), WIDE)
+        wait_bytes(act_two.at[num // 4, :, lanes], act_sem.at[num])
+        wait_bytes(slope_two.at[num // 4, :, lanes], slope_sem.at[num])
+        return carry
+
+    lax.fori_loop(0, DOZEN, finish, 0)
+
+    def finish_cast(k, carry):
+        wait_bytes(cast.at[k], cast_sem.at[k])
+        return carry
+
+    lax.fori_loop(0, 25, finish_cast, 0)
 
 
 def forward_and_grads(params, images, labels):
@@ -489,25 +490,30 @@
     return pl.pallas_call(
         grad_kernel,
         out_shape=[
-            jax.ShapeDtypeStruct((27, WIDE, WIDE), jnp.bfloat16),
+            jax.ShapeDtypeStruct((2, WIDE, WIDE), jnp.bfloat16),
+            jax.ShapeDtypeStruct((25, WIDE, WIDE), jnp.bfloat16),
+            jax.ShapeDtypeStruct((3, PAD_ROWS, 2048), jnp.bfloat16),
+            jax.ShapeDtypeStruct((3, PAD_ROWS, 2048), jnp.float32),
             jax.ShapeDtypeStruct((5, 4 * PAD_ROWS, THIN), jnp.bfloat16),
-            jax.ShapeDtypeStruct((4 * PAD_ROWS, THIN), jnp.bfloat16),
+            jax.ShapeDtypeStruct((3, PAD_ROWS, WIDE), jnp.bfloat16),
+            jax.ShapeDtypeStruct((PAD_ROWS, WIDE), jnp.bfloat16),
             jax.ShapeDtypeStruct((2, WIDE, WIDE), jnp.bfloat16),
         ],
         in_specs=[any_hbm] * 6 + [in_vmem, pl.BlockSpec(memory_space=pltpu.SMEM)],
-        out_specs=[any_hbm] + [in_vmem] * 3,
+        out_specs=[in_vmem] + [any_hbm] * 3 + [in_vmem] * 4,
         scratch_shapes=[
             pltpu.SemaphoreType.DMA((CHUNKS,)),
-            pltpu.SemaphoreType.DMA((RING,)),
+            pltpu.SemaphoreType.DMA((25,)),
+            pltpu.SemaphoreType.DMA((DOZEN,)),
+            pltpu.SemaphoreType.DMA((DOZEN,)),
             pltpu.VMEM((RING, WIDE, WIDE), jnp.float32),
-            pltpu.VMEM((RING, WIDE, WIDE), jnp.bfloat16),
             pltpu.VMEM((CHUNKS, WIDE, WIDE), jnp.bfloat16),
-            pltpu.VMEM((4, PAD_ROWS, WIDE), jnp.bfloat16),
-            pltpu.VMEM((3, PAD_ROWS, WIDE), jnp.bfloat16),
+            pltpu.VMEM((PAD_ROWS, WIDE), jnp.bfloat16),
+            pltpu.VMEM((PAD_ROWS, WIDE), jnp.bfloat16),
             pltpu.VMEM((3, PAD_ROWS, 2048), jnp.bfloat16),
             pltpu.VMEM((3, PAD_ROWS, 2048), jnp.float32),
-            pltpu.VMEM((PAD_ROWS, WIDE), jnp.bfloat16),
             pltpu.VMEM((PAD_ROWS, WIDE), jnp.float32),
+            pltpu.VMEM((2 * TOKENS, THIN), jnp.float32),
         ],
         compiler_params=pltpu.CompilerParams(vmem_limit_bytes=62 * 2**20),
         cost_estimate=pl.CostEstimate(flops=3 * 10**10, bytes_accessed=5 * 10**7, transcendentals=0),
@@ -526,23 +532,74 @@
     lax.fori_loop(0, 4, step, 0)
 
 
-TILE = 208
-TILES = OCT
+TILE = PAD_ROWS
+TILES = 4
 
 
 def reduce_kernel(*refs):
-    grads, w_in = refs[0], refs[1:7]
-    resid_saved, grad_in, cast_one = refs[7:10]
-    out, w_sums, g_sums = refs[10:13]
-    load_sem, out_sem, w_sem, w_buf, grad_one, up_total, down_total = refs[13:20]
-    bufs = refs[20:]
+    head_grads, w_cast, act_in, slope_in, w_in = refs[0], refs[1], refs[2], refs[3], refs[4:10]
+    resid_saved, resid_two, grad_in, cast_one = refs[10:14]
+    out, w_sums, g_sums = refs[14:17]
+    load_sem, cast_sem, act_sem, slope_sem, out_sem, w_sem, w_buf, act_buf, slope_buf, normed_two, grad_two, total, grad_one, up_total, down_total = refs[17:STEP]
+    bufs = refs[STEP:]
     grad_buf, full_buf = bufs[0:2]
 
-    def load(k, carry):
-        pltpu.make_async_copy(grads.at[k], grad_buf.at[k], load_sem.at[k]).start()
-        return carry
-
-    lax.fori_loop(0, 27, load, 0)
+    def load_cast(k, spot):
+        pltpu.make_async_copy(w_cast.at[spot], full_buf.at[k], cast_sem.at[spot]).start()
+
+    def load_saved(num):
+        layer = 2 - num // 4
+        lanes = pl.ds(pl.multiple_of((num % 4) * WIDE, WIDE), WIDE)
+        pltpu.make_async_copy(act_in.at[layer, :, lanes], act_buf.at[num % 2], act_sem.at[num]).start()
+        pltpu.make_async_copy(slope_in.at[layer, :, lanes], slope_buf.at[num % 2], slope_sem.at[num]).start()
+
+    def load_pair(num, carry):
+        base = (num // 4) * OCT + num % 4
+        load_cast(base, base)
+        load_cast(base + 4, base + 4)
+        @pl.when(num < 2)
+        def _():
+            load_saved(num)
+        return carry
+
+    lax.fori_loop(0, DOZEN, load_pair, 0)
+    load_cast(MERGE, TWO_CHUNKS)
+    for k in range(2):
+        pltpu.make_async_copy(head_grads.at[k], grad_buf.at[HEAD_A + k], load_sem.at[k]).start()
+    grad_two[...] = grad_in[...]
+
+    def two_backward(num):
+        layer, part = 2 - num // 4, num % 4
+        base = (num // 4) * OCT + part
+        slot = num % 2
+        for k in range(2):
+            wait_bytes(full_buf.at[base + 4 * k], cast_sem.at[base + 4 * k])
+        wait_bytes(act_buf.at[slot], act_sem.at[num])
+        wait_bytes(slope_buf.at[slot], slope_sem.at[num])
+        @pl.when(part == 0)
+        def _():
+            normed_two[...] = layer_norm(resid_two[layer].astype(jnp.float32)).astype(jnp.bfloat16)
+            total[...] = jnp.zeros_like(total)
+        grad_buf[base] = dot_rows(act_buf[slot], grad_two[...]).astype(jnp.bfloat16)
+        grad_pre = (dot_cols(grad_two[...], full_buf[base]) * slope_buf[slot]).astype(jnp.bfloat16)
+        grad_buf[base + 4] = dot_rows(normed_two[...], grad_pre).astype(jnp.bfloat16)
+        total[...] += dot_cols(grad_pre, full_buf[base + 4])
+        @pl.when(part == 3)
+        def _():
+            normed, inverse = layer_norm_parts(resid_two[layer].astype(jnp.float32))
+            back = layer_norm_back(total[...], normed, inverse) + grad_two[...].astype(jnp.float32)
+            grad_two[...] = back.astype(jnp.bfloat16)
+        @pl.when(num < 10)
+        def _():
+            load_saved(num + 2)
+
+    def merge_backward():
+        wait_bytes(full_buf.at[MERGE], cast_sem.at[TWO_CHUNKS])
+        for part in range(4):
+            rows = slice(part * PAD_ROWS, (part + 1) * PAD_ROWS)
+            spots = slice(part * THIN, (part + 1) * THIN)
+            grad_buf[MERGE, spots, :] = dot_rows(resid_saved[4, rows, :], grad_two[...]).astype(jnp.bfloat16)
+            grad_one[rows, :] = dot_cols(grad_two[...], full_buf[MERGE, spots, :]).astype(jnp.bfloat16)
 
     def w_start(k):
         two_copies(k, w_in[3], w_in[4], w_buf.at[k % W_RING], w_sem.at[k], True)
@@ -553,7 +610,6 @@
 
     for k in range(W_RING):
         w_start(jnp.int32(k))
-    grad_one[...] = grad_in[...]
 
     def one_backward(num, carry):
         layer, tile = 3 - num // TILES, num % TILES
@@ -580,9 +636,17 @@
     up_total[...] = jnp.zeros_like(up_total)
 
     def each_tick(t):
-        @pl.when(t < PAIR)
-        def _():
-            lax.fori_loop(t * 2, t * 2 + 2, one_backward, 0)
+        @pl.when(t < DOZEN)
+        def _():
+            two_backward(t)
+
+        @pl.when(t == DOZEN)
+        def _():
+            merge_backward()
+
+        @pl.when((t >= DOZEN) & (t < 28))
+        def _():
+            one_backward(t - DOZEN, 0)
 
         @pl.when(t < TWO_CHUNKS)
         def _():
@@ -606,9 +670,10 @@
                 w_sum(k)
 
     def before(k):
-        @pl.when(k < 27)
-        def _():
-            wait_bytes(grad_buf.at[k], load_sem.at[k])
+        for num in range(2):
+            @pl.when(k == HEAD_A + num)
+            def _(num=num):
+                wait_bytes(grad_buf.at[HEAD_A + num], load_sem.at[num])
 
     def after(k):
         pltpu.make_async_copy(full_buf.at[k], out.at[k], out_sem.at[k]).start()
@@ -623,31 +688,42 @@
     lax.fori_loop(0, CHUNKS, finish, 0)
 
 
-def reduce_grads(grads, params, resid_saved, grad_one, cast_one):
+def reduce_grads(saved, params):
     any_hbm = pl.BlockSpec(memory_space=pltpu.HBM)
     in_vmem = pl.BlockSpec(memory_space=pltpu.VMEM)
     sums_shape = (CHUNKS, 4, LANES)
     return pl.pallas_call(
         reduce_kernel,
         out_shape=[jax.ShapeDtypeStruct((CHUNKS, WIDE, WIDE), jnp.bfloat16)] + [jax.ShapeDtypeStruct(sums_shape, jnp.float32)] * 2,
-        in_specs=[any_hbm] * 7 + [in_vmem] * 3,
+        in_specs=[any_hbm] * 10 + [in_vmem] * 4,
         out_specs=[any_hbm] + [in_vmem] * 2,
-        scratch_shapes=[pltpu.SemaphoreType.DMA((CHUNKS,))] * 3 + [
+        scratch_shapes=[
+            pltpu.SemaphoreType.DMA((2,)),
+            pltpu.SemaphoreType.DMA((25,)),
+            pltpu.SemaphoreType.DMA((DOZEN,)),
+            pltpu.SemaphoreType.DMA((DOZEN,)),
+            pltpu.SemaphoreType.DMA((CHUNKS,)),
+            pltpu.SemaphoreType.DMA((CHUNKS,)),
             pltpu.VMEM((W_RING, WIDE, WIDE), jnp.float32),
+            pltpu.VMEM((2, PAD_ROWS, WIDE), jnp.bfloat16),
+            pltpu.VMEM((2, PAD_ROWS, WIDE), jnp.float32),
+            pltpu.VMEM((PAD_ROWS, WIDE), jnp.bfloat16),
+            pltpu.VMEM((PAD_ROWS, WIDE), jnp.bfloat16),
+            pltpu.VMEM((PAD_ROWS, WIDE), jnp.float32),
             pltpu.VMEM((4 * PAD_ROWS, THIN), jnp.bfloat16),
             pltpu.VMEM((THIN, WIDE), jnp.float32),
             pltpu.VMEM((WIDE, THIN), jnp.float32),
         ] + scratch(CHUNKS, WIDE),
         compiler_params=pltpu.CompilerParams(has_side_effects=True, vmem_limit_bytes=62 * 2**20),
         cost_estimate=pl.CostEstimate(flops=10**10, bytes_accessed=6 * 10**7, transcendentals=0),
-    )(grads, *params, resid_saved, grad_one, cast_one)
+    )(*saved[0:4], *params, *saved[4:OCT])
 
 
 def next_kernel(*refs):
     grads, w_in, v_in = refs[0], refs[1:7], refs[7:13]
     w_sums, g_sums, images = refs[13:PAIR]
     logits, w_out, v_out = refs[PAIR], refs[17:23], refs[23:29]
-    load_sem, store_sem, ring_w, ring_v, ring_g, cast, coef, resid_one, resid_two, normed_two, total_two = refs[29:]
+    load_sem, store_sem, ring_w, ring_v, ring_g, cast, coef, resid_one, resid_two, normed_two, total_two, wide = refs[29:]
     rings = (ring_w, ring_v)
 
     def start_small(num):
@@ -672,7 +748,7 @@
     def total(sums, first, size):
         return jnp.sum(jnp.sum(jnp.sum(sums[first:first + size], axis=0), axis=0, keepdims=True), axis=1, keepdims=True)
 
-    for first, size in [(0, 4), (4, 4), (OCT, 4), (12, 4), (PAIR, 4), (20, 4), (HEAD_A, 2), (MERGE, 1)]:
+    for first, size in [(0, 4), (4, 4), (OCT, 4), (DOZEN, 4), (PAIR, 4), (20, 4), (HEAD_A, 2), (MERGE, 1)]:
         value = ratio(total(w_sums, first, size), total(g_sums, first, size))
         for k in range(first, first + size):
             coef[k] = jnp.broadcast_to(value, (4, LANES))
@@ -739,7 +815,7 @@
         start_two(num)
     for num in range(5):
         update_small(num)
-    resid_one[...] = images[...]
+    arrange(images, wide, resid_one)
     wait_small_store(0)
     start_two(3)
 
@@ -775,19 +851,12 @@
             resid_two[...] = (resid_two[...].astype(jnp.float32) + total_two[...]).astype(jnp.bfloat16)
         return carry
 
-    lax.fori_loop(0, 12, second, 0)
+    lax.fori_loop(0, DOZEN, second, 0)
     head_in = layer_norm(pool_images(resid_two)).astype(jnp.bfloat16)
     logits[:, 0:WIDE] = dot_cols(head_in, cast[HEAD_A])[0:2]
     logits[:, WIDE:1000] = dot_cols(head_in, cast[HEAD_B])[0:2, 0:HEAD_REST]
     for num in range(PAIR, TWO_CHUNKS):
         wait_two_store(num)
-
-
-def arrange(images):
-    count, tokens, width = images.shape
-    split = images.reshape(count, tokens // 4, 4, width).transpose(2, 0, 1, 3)
-    split = jnp.pad(split, ((0, 0), (0, 0), (0, PAD_IMG - tokens // 4), (0, 0)))
-    return split.reshape(4 * count * PAD_IMG, width)
 
 
 def update_and_forward(params, velocities, grads, w_sums, g_sums, images):
@@ -798,7 +867,7 @@
         next_kernel,
         out_shape=[jax.ShapeDtypeStruct((2, CLASSES), jnp.float32)] + shapes + shapes,
         in_specs=[any_hbm] * 13 + [in_vmem] * 3,
-        out_specs=[in_vmem] + [any_hbm] * 12,
+        out_specs=[in_vmem] + [any_hbm] * DOZEN,
         scratch_shapes=[
             pltpu.SemaphoreType.DMA((3, CHUNKS)),
             pltpu.SemaphoreType.DMA((2, CHUNKS)),
@@ -811,6 +880,7 @@
             pltpu.VMEM((PAD_ROWS, WIDE), jnp.bfloat16),
             pltpu.VMEM((PAD_ROWS, WIDE), jnp.bfloat16),
             pltpu.VMEM((PAD_ROWS, WIDE), jnp.float32),
+            pltpu.VMEM((2 * TOKENS, THIN), jnp.float32),
         ],
         compiler_params=pltpu.CompilerParams(vmem_limit_bytes=58 * 2**20),
         cost_estimate=pl.CostEstimate(flops=10**10, bytes_accessed=135 * 10**6, transcendentals=0),
@@ -822,14 +892,14 @@
     def local_step(x_now, labels_now, x_next, *weights):
         params = weights[0:5] + (weights[5].T,)
         velocities = weights[6:11] + (weights[11].T,)
-        grads, resid_saved, grad_one, cast_one = forward_and_grads(params, arrange(x_now), labels_now)
-        sums, w_sums, g_sums = reduce_grads(grads, params, resid_saved, grad_one, cast_one)
-        outs = update_and_forward(params, velocities, sums, w_sums, g_sums, arrange(x_next))
+        saved = forward_and_grads(params, x_now, labels_now)
+        sums, w_sums, g_sums = reduce_grads(saved, params)
+        outs = update_and_forward(params, velocities, sums, w_sums, g_sums, x_next)
         new_w, new_v = outs[1:7], outs[7:13]
         return (outs[0],) + tuple(new_w[0:5]) + (new_w[5].T,) + tuple(new_v[0:5]) + (new_v[5].T,)
 
     replicated = P()
     batch_split = P('data')
-    in_specs = (batch_split, batch_split, batch_split) + (replicated,) * 12
-    out_specs = (batch_split,) + (replicated,) * 12
+    in_specs = (batch_split, batch_split, batch_split) + (replicated,) * DOZEN
+    out_specs = (batch_split,) + (replicated,) * DOZEN
     return jax.shard_map(local_step, mesh=mesh, in_specs=in_specs, out_specs=out_specs, check_vma=False)

time: 265 us -> 238 us (0.90)
  Pallas kernels: 261 us -> 237 us
  local copies, waits for them, and re-layouts: 3.7 us -> 0 us
    pallas_call x1, Pallas kernels: 59.4 us -> 37.6 us  [forward_and_grads(): pl.pallas_call(grad_kernel, out_shape=[jax.ShapeDtypeStruct((2, WIDE, WID...]
where the time goes in v3:
time: 238 us
  Pallas kernels  237 us (100%)
    pallas_call x1, Pallas kernels, reduce_grads(): pl.pallas_call(reduce_kernel, out_shape=[jax.ShapeDtypeStruct((CHUNKS, WI...  145 us
    pallas_call x1, Pallas kernels, update_and_forward(): pl.pallas_call(next_kernel, out_shape=[jax.ShapeDtypeStruct((2, CLASSES),...  54.7 us
    pallas_call x1, Pallas kernels, forward_and_grads(): pl.pallas_call(grad_kernel, out_shape=[jax.ShapeDtypeStruct((2, WIDE, WID...  37.6 us

profile of v3, /device:TPU:0, one launch (start us, length us, event | category | flops | bytes accessed | tf_op | source)
XLA Modules:
  0.0 238.2 jit_solution(8978672776188625970)
XLA Ops:
  0.6 37.6 %shard_map.246 = (bf16[2,512,512]{2,1,0:T(8,128)(2,1)}, bf16[25,512,512]{2,1,0:T(8,128)(2,1)}, bf16[3,416,2048]{2,1,0:T(8,128)(2,1)}, f32[3,416,2048]{2,1,0:T(8,...) custom-call(f32[4,128,512]{2,1,0:T(8,128)} %refs_1_.3, ...), custom_call_target="tpu_custom_call" | custom-call | flops 30000001024 | bytes 50000000 | tf_op jit(solution)/shard_map/pallas_call | solution.py:490
  38.3 145.1 %shard_map.247 = (bf16[29,512,512]{2,1,0:T(8,128)(2,1)}, f32[29,4,512]{2,1,0:T(4,128)}, f32[29,4,512]{2,1,0:T(4,128)}) custom-call(bf16[2,512,512]{2,1,0:T(8,128)(2,1)} %get-tuple-element.37.refs_0_, bf16[25,512,512]{2,1,0:T(8,128)(2,1)} %get-tuple-element.38.refs_1_, bf16[3,416,2048]{2,1,0:T(8,128)(2,1)} %get-tuple-element.39.refs_2_, ...), custom_call_target="tpu_custom_call" | custom-call | flops 10000000000 | bytes 60000000 | tf_op jit(solution)/shard_map/pallas_call | solution.py:695
  183.3 54.7 %shard_map.248 = (f32[2,1000]{1,0:T(2,128)}, f32[4,128,512]{2,1,0:T(8,128)}, f32[4,512,128]{2,1,0:T(8,128)}, f32[512,512]{1,0:T(8,128)}, f32[3,512,2048]{2,1,0:T...) custom-call(bf16[29,512,512]{2,1,0:T(8,128)(2,1)} %get-tuple-element, ...), custom_call_target="tpu_custom_call" | custom-call | flops 10000000000 | bytes 135000000 | tf_op jit(solution)/shard_map/pallas_call | solution.py:866

commit v4 on v3

--- a/solution.py
+++ b/solution.py
@@ -33,11 +33,11 @@
 OCT = 8
 PAIR = 16
 DOZEN = 12
+SMALL_COUNT = 5
+CASTS = 25
 
 MESH = pl.DeviceIdType.MESH
-ROWS = WIDE
-LAG = 3
-STAGES = DOZEN
+OFFSETS = tuple(2 * num + (num >= 2) + (num >= 11) for num in range(13))
 
 
 def all_reduce_body(chunks, grad_buf, full_buf, recv_core, recv_one, recv_z, recv_mid, recv_two, send_sem, recv_sem, before, after, extra):
@@ -99,7 +99,7 @@
         return remote(rows(k, near + (1 - two) * STEP, STEP), recv_two.at[k], 4, k, dev_two)
 
     def g_two(k):
-        return remote(full(k, mine, STEP), full(k, mine, STEP), 5, k, dev_two)
+        return remote(full(k, mine, STEP), full(k, mine, STEP), SMALL_COUNT, k, dev_two)
 
     def g_in(k):
         return remote(full(k, near, QUARTER), full(k, near, QUARTER), 6, k, dev_inner)
@@ -211,11 +211,11 @@
         for num, stage in reversed(list(enumerate(stages))):
             if num == 0:
                 extra(t)
-            k = t - num * LAG
+            k = t - OFFSETS[num]
             pl.when((k >= 0) & (k < chunks))(functools.partial(stage, k))
         return carry
 
-    lax.fori_loop(0, chunks + STAGES * LAG, tick, 0)
+    lax.fori_loop(0, chunks + OFFSETS[-1], tick, 0)
 
 
 def scratch(chunks, cols):
@@ -289,7 +289,7 @@
 
 
 def small_pieces(k, arrays):
-    up_one, down_one, merge, head = arrays[0], arrays[1], arrays[2], arrays[5]
+    up_one, down_one, merge, head = arrays[0], arrays[1], arrays[2], arrays[SMALL_COUNT]
     if k == UP_ONE:
         return [(up_one.at[layer], (pl.ds(layer * THIN, THIN),)) for layer in range(4)]
     if k == DOWN_ONE:
@@ -319,7 +319,7 @@
 
 
 def two_item(num):
-    return (2 - num // OCT) * OCT + (num + 4) % OCT
+    return (2 - num // OCT) * OCT + (1 - num % 2) * 4 + (num % OCT) // 2
 
 
 def one_forward(num, resid_in, resid_out, cast):
@@ -369,14 +369,14 @@
 
     def start_two(num):
         k = two_item(num)
-        two_copies(k, w_in[3], w_in[4], ring_w.at[(num + 5) % RING], load_sem.at[k], True)
+        two_copies(k, w_in[3], w_in[4], ring_w.at[(num + SMALL_COUNT) % RING], load_sem.at[k], True)
 
     def cast_slot(k, slot):
         def step(num, carry):
-            rows = pl.ds(pl.multiple_of(num * QUARTER, QUARTER), QUARTER)
+            rows = pl.ds(pl.multiple_of(num * THIN, THIN), THIN)
             cast[k, rows, :] = ring_w[slot, rows, :].astype(jnp.bfloat16)
             return carry
-        lax.fori_loop(0, OCT, step, 0)
+        lax.fori_loop(0, 4, step, 0)
 
     def cast_small(num):
         k = SMALL_ORDER[num]
@@ -387,7 +387,7 @@
 
     def cast_two(num):
         k = two_item(num)
-        slot = (num + 5) % RING
+        slot = (num + SMALL_COUNT) % RING
         wait_bytes(ring_w.at[slot], load_sem.at[k])
         cast_slot(k, slot)
         send_cast(k, k)
@@ -395,17 +395,17 @@
         def _():
             start_two(num + RING)
 
-    for num in range(5):
+    for num in range(SMALL_COUNT):
         start_small(num)
     for num in range(3):
         start_two(num)
-    for num in range(5):
+    arrange(images, wide, resid_saved.at[0])
+    for num in range(SMALL_COUNT):
         cast_small(num)
         start_two(num + 3)
     send_cast(MERGE, TWO_CHUNKS)
     cast_one[0] = cast[DOWN_ONE]
     cast_one[1] = cast[UP_ONE]
-    arrange(images, wide, resid_saved.at[0])
 
     def first(num, carry):
         layer = num // 4
@@ -481,7 +481,7 @@
         wait_bytes(cast.at[k], cast_sem.at[k])
         return carry
 
-    lax.fori_loop(0, 25, finish_cast, 0)
+    lax.fori_loop(0, CASTS, finish_cast, 0)
 
 
 def forward_and_grads(params, images, labels):
@@ -491,10 +491,10 @@
         grad_kernel,
         out_shape=[
             jax.ShapeDtypeStruct((2, WIDE, WIDE), jnp.bfloat16),
-            jax.ShapeDtypeStruct((25, WIDE, WIDE), jnp.bfloat16),
+            jax.ShapeDtypeStruct((CASTS, WIDE, WIDE), jnp.bfloat16),
             jax.ShapeDtypeStruct((3, PAD_ROWS, 2048), jnp.bfloat16),
             jax.ShapeDtypeStruct((3, PAD_ROWS, 2048), jnp.float32),
-            jax.ShapeDtypeStruct((5, 4 * PAD_ROWS, THIN), jnp.bfloat16),
+            jax.ShapeDtypeStruct((SMALL_COUNT, 4 * PAD_ROWS, THIN), jnp.bfloat16),
             jax.ShapeDtypeStruct((3, PAD_ROWS, WIDE), jnp.bfloat16),
             jax.ShapeDtypeStruct((PAD_ROWS, WIDE), jnp.bfloat16),
             jax.ShapeDtypeStruct((2, WIDE, WIDE), jnp.bfloat16),
@@ -503,7 +503,7 @@
         out_specs=[in_vmem] + [any_hbm] * 3 + [in_vmem] * 4,
         scratch_shapes=[
             pltpu.SemaphoreType.DMA((CHUNKS,)),
-            pltpu.SemaphoreType.DMA((25,)),
+            pltpu.SemaphoreType.DMA((CASTS,)),
             pltpu.SemaphoreType.DMA((DOZEN,)),
             pltpu.SemaphoreType.DMA((DOZEN,)),
             pltpu.VMEM((RING, WIDE, WIDE), jnp.float32),
@@ -516,7 +516,7 @@
             pltpu.VMEM((2 * TOKENS, THIN), jnp.float32),
         ],
         compiler_params=pltpu.CompilerParams(vmem_limit_bytes=62 * 2**20),
-        cost_estimate=pl.CostEstimate(flops=3 * 10**10, bytes_accessed=5 * 10**7, transcendentals=0),
+        cost_estimate=pl.CostEstimate(flops=3 * 10**10, bytes_accessed=SMALL_COUNT * 10**7, transcendentals=0),
     )(*params, images, labels)
 
 
@@ -699,7 +699,7 @@
         out_specs=[any_hbm] + [in_vmem] * 2,
         scratch_shapes=[
             pltpu.SemaphoreType.DMA((2,)),
-            pltpu.SemaphoreType.DMA((25,)),
+            pltpu.SemaphoreType.DMA((CASTS,)),
             pltpu.SemaphoreType.DMA((DOZEN,)),
             pltpu.SemaphoreType.DMA((DOZEN,)),
             pltpu.SemaphoreType.DMA((CHUNKS,)),
@@ -734,13 +734,15 @@
 
     def start_two(num):
         k = two_item(num)
-        slot = (num + 5) % RING
+        slot = (num + SMALL_COUNT) % RING
         for which, arrays in enumerate((w_in, v_in)):
             two_copies(k, arrays[3], arrays[4], rings[which].at[slot], load_sem.at[which, k], True)
         pltpu.make_async_copy(grads.at[k], ring_g.at[slot], load_sem.at[2, k]).start()
 
-    for num in range(5):
+    for num in range(SMALL_COUNT):
         start_small(num)
+    for num in range(3):
+        start_two(num)
 
     def ratio(w_total, g_total):
         return TRUST * (jnp.sqrt(w_total) / jnp.sqrt(g_total))
@@ -761,15 +763,15 @@
 
     def apply_update(k, slot):
         def step(num, carry):
-            rows = pl.ds(pl.multiple_of(num * STEP, STEP), STEP)
-            factor = coef[k, pl.ds(num // 4, 1), :]
+            rows = pl.ds(pl.multiple_of(num * QUARTER, QUARTER), QUARTER)
+            factor = coef[k, pl.ds(num // 2, 1), :]
             new_v = MOMENTUM * ring_v[slot, rows, :] + factor * ring_g[slot, rows, :].astype(jnp.float32)
             new_w = ring_w[slot, rows, :] - new_v
             ring_v[slot, rows, :] = new_v
             ring_w[slot, rows, :] = new_w
             cast[k, rows, :] = new_w.astype(jnp.bfloat16)
             return carry
-        lax.fori_loop(0, PAIR, step, 0)
+        lax.fori_loop(0, OCT, step, 0)
 
     def update_small(num):
         k = SMALL_ORDER[num]
@@ -789,13 +791,13 @@
 
     def wait_two_store(num):
         k = two_item(num)
-        slot = (num + 5) % RING
+        slot = (num + SMALL_COUNT) % RING
         for which in range(2):
             wait_bytes(rings[which].at[slot], store_sem.at[which, k])
 
     def update_two(num, carry):
         k = two_item(num)
-        slot = (num + 5) % RING
+        slot = (num + SMALL_COUNT) % RING
         for which in range(2):
             wait_bytes(rings[which].at[slot], load_sem.at[which, k])
         wait_bytes(ring_g.at[slot], load_sem.at[2, k])
@@ -811,16 +813,14 @@
             start_two(later)
         return carry
 
-    for num in range(3):
-        start_two(num)
-    for num in range(5):
+    arrange(images, wide, resid_one)
+    for num in range(SMALL_COUNT):
         update_small(num)
-    arrange(images, wide, resid_one)
     wait_small_store(0)
     start_two(3)
 
     def first(num, carry):
-        for small in range(1, 5):
+        for small in range(1, SMALL_COUNT):
             @pl.when(num == small - 1)
             def _(small=small):
                 wait_small_store(small)
@@ -835,23 +835,26 @@
     lax.fori_loop(0, OCT, first, 0)
     merge_forward(resid_one, cast, resid_two)
 
-    def second(num, carry):
+    def two_forward(num):
         layer, part = num // 4, num % 4
         @pl.when(part == 0)
         def _():
             normed_two[...] = layer_norm(resid_two[...].astype(jnp.float32)).astype(jnp.bfloat16)
             total_two[...] = jnp.zeros_like(total_two)
-        @pl.when(layer < 2)
-        def _():
-            lax.fori_loop(OCT + num * 2, 10 + num * 2, update_two, 0)
         act = gelu(dot_plain(normed_two[...], cast[(2 - layer) * OCT + 4 + part])).astype(jnp.bfloat16)
         total_two[...] += dot_plain(act, cast[(2 - layer) * OCT + part])
         @pl.when(part == 3)
         def _():
             resid_two[...] = (resid_two[...].astype(jnp.float32) + total_two[...]).astype(jnp.bfloat16)
-        return carry
-
-    lax.fori_loop(0, DOZEN, second, 0)
+
+    def second(num, carry):
+        update_two(num + OCT, 0)
+        @pl.when((num < OCT) | (num % 2 == 1))
+        def _():
+            two_forward(jnp.minimum(num, OCT) + jnp.maximum(num - OCT, 0) // 2)
+        return carry
+
+    lax.fori_loop(0, PAIR, second, 0)
     head_in = layer_norm(pool_images(resid_two)).astype(jnp.bfloat16)
     logits[:, 0:WIDE] = dot_cols(head_in, cast[HEAD_A])[0:2]
     logits[:, WIDE:1000] = dot_cols(head_in, cast[HEAD_B])[0:2, 0:HEAD_REST]
@@ -890,13 +893,13 @@
 
 def solution(mesh):
     def local_step(x_now, labels_now, x_next, *weights):
-        params = weights[0:5] + (weights[5].T,)
+        params = weights[0:SMALL_COUNT] + (weights[SMALL_COUNT].T,)
         velocities = weights[6:11] + (weights[11].T,)
         saved = forward_and_grads(params, x_now, labels_now)
         sums, w_sums, g_sums = reduce_grads(saved, params)
         outs = update_and_forward(params, velocities, sums, w_sums, g_sums, x_next)
         new_w, new_v = outs[1:7], outs[7:13]
-        return (outs[0],) + tuple(new_w[0:5]) + (new_w[5].T,) + tuple(new_v[0:5]) + (new_v[5].T,)
+        return (outs[0],) + tuple(new_w[0:SMALL_COUNT]) + (new_w[SMALL_COUNT].T,) + tuple(new_v[0:SMALL_COUNT]) + (new_v[SMALL_COUNT].T,)
 
     replicated = P()
     batch_split = P('data')

time: 238 us -> 230 us (0.966)
  Pallas kernels: 237 us -> 229 us
    pallas_call x1, Pallas kernels: 54.7 us -> 50.7 us  [update_and_forward(): pl.pallas_call(next_kernel, out_shape=[jax.ShapeDtypeStruct((2, CLASSES),...]
    pallas_call x1, Pallas kernels: 145 us -> 142 us  [reduce_grads(): pl.pallas_call(reduce_kernel, out_shape=[jax.ShapeDtypeStruct((CHUNKS, WI...]
where the time goes in v4:
time: 230 us
  Pallas kernels  229 us (100%)
    pallas_call x1, Pallas kernels, reduce_grads(): pl.pallas_call(reduce_kernel, out_shape=[jax.ShapeDtypeStruct((CHUNKS, WI...  142 us
    pallas_call x1, Pallas kernels, update_and_forward(): pl.pallas_call(next_kernel, out_shape=[jax.ShapeDtypeStruct((2, CLASSES),...  50.7 us
    pallas_call x1, Pallas kernels, forward_and_grads(): pl.pallas_call(grad_kernel, out_shape=[jax.ShapeDtypeStruct((2, WIDE, WID...  37.1 us

profile of v4, /device:TPU:0, one launch (start us, length us, event | category | flops | bytes accessed | tf_op | source)
XLA Modules:
  0.0 230.3 jit_solution(16779012714180793178)
XLA Ops:
  0.6 37.1 %shard_map.246 = (bf16[2,512,512]{2,1,0:T(8,128)(2,1)}, bf16[25,512,512]{2,1,0:T(8,128)(2,1)}, bf16[3,416,2048]{2,1,0:T(8,128)(2,1)}, f32[3,416,2048]{2,1,0:T(8,...) custom-call(f32[4,128,512]{2,1,0:T(8,128)} %refs_1_.3, ...), custom_call_target="tpu_custom_call" | custom-call | flops 30000001024 | bytes 50000000 | tf_op jit(solution)/shard_map/pallas_call | solution.py:490
  37.8 141.7 %shard_map.247 = (bf16[29,512,512]{2,1,0:T(8,128)(2,1)}, f32[29,4,512]{2,1,0:T(4,128)}, f32[29,4,512]{2,1,0:T(4,128)}) custom-call(bf16[2,512,512]{2,1,0:T(8,128)(2,1)} %get-tuple-element.37.refs_0_, bf16[25,512,512]{2,1,0:T(8,128)(2,1)} %get-tuple-element.38.refs_1_, bf16[3,416,2048]{2,1,0:T(8,128)(2,1)} %get-tuple-element.39.refs_2_, ...), custom_call_target="tpu_custom_call" | custom-call | flops 10000000000 | bytes 60000000 | tf_op jit(solution)/shard_map/pallas_call | solution.py:695
  179.5 50.7 %shard_map.248 = (f32[2,1000]{1,0:T(2,128)}, f32[4,128,512]{2,1,0:T(8,128)}, f32[4,512,128]{2,1,0:T(8,128)}, f32[512,512]{1,0:T(8,128)}, f32[3,512,2048]{2,1,0:T...) custom-call(bf16[29,512,512]{2,1,0:T(8,128)(2,1)} %get-tuple-element, ...), custom_call_target="tpu_custom_call" | custom-call | flops 10000000000 | bytes 135000000 | tf_op jit(solution)/shard_map/pallas_call | solution.py:869

commit v5 on v4

--- a/solution.py
+++ b/solution.py
@@ -22,6 +22,7 @@
 TOKENS = 784
 PAD_IMG = 208
 PAD_ROWS = 416
+TALL = 1664
 GELU_C = 0.7978845608028654
 GELU_A = 0.044715
 WIDE = 512
@@ -37,7 +38,7 @@
 CASTS = 25
 
 MESH = pl.DeviceIdType.MESH
-OFFSETS = tuple(2 * num + (num >= 2) + (num >= 11) for num in range(13))
+OFFSETS = tuple(2 * num + (num >= 2) + 2 * (num >= 11) for num in range(13))
 
 
 def all_reduce_body(chunks, grad_buf, full_buf, recv_core, recv_one, recv_z, recv_mid, recv_two, send_sem, recv_sem, before, after, extra):
@@ -323,8 +324,8 @@
 
 
 def one_forward(num, resid_in, resid_out, cast):
-    layer = num // 4
-    rows = pl.ds(pl.multiple_of((num % 4) * PAD_ROWS, STEP), PAD_ROWS)
+    layer = num // 1
+    rows = pl.ds(pl.multiple_of((num % 1) * TALL, STEP), TALL)
     lanes = pl.ds(pl.multiple_of(layer * THIN, THIN), THIN)
     resid = resid_in[rows, :].astype(jnp.float32)
     normed = layer_norm(resid).astype(jnp.bfloat16)
@@ -408,33 +409,42 @@
     cast_one[1] = cast[UP_ONE]
 
     def first(num, carry):
-        layer = num // 4
+        layer = num // 1
         one_forward(num, resid_saved.at[layer], resid_saved.at[layer + 1], cast)
-        cast_two(num)
-        return carry
-
-    lax.fori_loop(0, PAIR, first, 0)
+        for extra in range(4):
+            cast_two(4 * num + extra)
+        return carry
+
+    lax.fori_loop(0, 4, first, 0)
     merge_forward(resid_saved.at[4], cast, resid_two.at[0])
 
     def second(num, carry):
-        layer, part = num // 4, num % 4
-        lanes = pl.ds(pl.multiple_of(part * WIDE, WIDE), WIDE)
-        @pl.when(part == 0)
+        layer = num // 2
+        @pl.when(num % 2 == 0)
         def _():
             normed_two[...] = layer_norm(resid_two[layer].astype(jnp.float32)).astype(jnp.bfloat16)
             total[...] = jnp.zeros_like(total)
-        @pl.when(num < OCT)
-        def _():
-            cast_two(num + PAIR)
-        pre = dot_plain(normed_two[...], cast[(2 - layer) * OCT + 4 + part])
-        act, slope = gelu_and_slope(pre)
-        act = act.astype(jnp.bfloat16)
-        act_two[layer, :, lanes] = act
-        slope_two[layer, :, lanes] = slope
-        total[...] += dot_plain(act, cast[(2 - layer) * OCT + part])
-        pltpu.make_async_copy(act_two.at[layer, :, lanes], act_out.at[layer, :, lanes], act_sem.at[num]).start()
-        pltpu.make_async_copy(slope_two.at[layer, :, lanes], slope_out.at[layer, :, lanes], slope_sem.at[num]).start()
-        @pl.when(part == 3)
+        @pl.when(num < 4)
+        def _():
+            cast_two(2 * num + PAIR)
+            cast_two(2 * num + PAIR + 1)
+        value = total[...]
+        for sub in range(2):
+            part = 2 * (num % 2) + sub
+            lanes = pl.ds(pl.multiple_of(part * WIDE, WIDE), WIDE)
+            pre = dot_plain(normed_two[...], cast[(2 - layer) * OCT + 4 + part])
+            act, slope = gelu_and_slope(pre)
+            act = act.astype(jnp.bfloat16)
+            act_two[layer, :, lanes] = act
+            slope_two[layer, :, lanes] = slope
+            value = value + dot_plain(act, cast[(2 - layer) * OCT + part])
+        total[...] = value
+        for sub in range(2):
+            part = 2 * (num % 2) + sub
+            lanes = pl.ds(pl.multiple_of(part * WIDE, WIDE), WIDE)
+            pltpu.make_async_copy(act_two.at[layer, :, lanes], act_out.at[layer, :, lanes], act_sem.at[2 * num + sub]).start()
+            pltpu.make_async_copy(slope_two.at[layer, :, lanes], slope_out.at[layer, :, lanes], slope_sem.at[2 * num + sub]).start()
+        @pl.when(num % 2 == 1)
         def _():
             value = (resid_two[layer].astype(jnp.float32) + total[...]).astype(jnp.bfloat16)
             @pl.when(layer < 2)
@@ -445,7 +455,7 @@
                 last_two[...] = value
         return carry
 
-    lax.fori_loop(0, DOZEN, second, 0)
+    lax.fori_loop(0, 6, second, 0)
 
     pooled = pool_images(last_two)
     head_norm, head_inv = layer_norm_parts(pooled)
@@ -826,11 +836,10 @@
                 wait_small_store(small)
         update_two(num, 0)
 
-        def body(part, carry):
-            one_forward(part, resid_one, resid_one, cast)
-            return carry
-
-        return lax.fori_loop(num * 2, num * 2 + 2, body, carry)
+        @pl.when(num % 2 == 1)
+        def _():
+            one_forward(num // 2, resid_one, resid_one, cast)
+        return carry
 
     lax.fori_loop(0, OCT, first, 0)
     merge_forward(resid_one, cast, resid_two)

time: 230 us -> 222 us (0.965)
  Pallas kernels: 229 us -> 221 us
    pallas_call x1, Pallas kernels: 37.1 us -> 32 us  [forward_and_grads(): pl.pallas_call(grad_kernel, out_shape=[jax.ShapeDtypeStruct((2, WIDE, WID...]
    pallas_call x1, Pallas kernels: 50.7 us -> 47.9 us  [update_and_forward(): pl.pallas_call(next_kernel, out_shape=[jax.ShapeDtypeStruct((2, CLASSES),...]
where the time goes in v5:
time: 222 us
  Pallas kernels  221 us (100%)
    pallas_call x1, Pallas kernels, reduce_grads(): pl.pallas_call(reduce_kernel, out_shape=[jax.ShapeDtypeStruct((CHUNKS, WI...  141 us
    pallas_call x1, Pallas kernels, update_and_forward(): pl.pallas_call(next_kernel, out_shape=[jax.ShapeDtypeStruct((2, CLASSES),...  47.9 us
    pallas_call x1, Pallas kernels, forward_and_grads(): pl.pallas_call(grad_kernel, out_shape=[jax.ShapeDtypeStruct((2, WIDE, WID...  32 us

profile of v5, /device:TPU:0, one launch (start us, length us, event | category | flops | bytes accessed | tf_op | source)
XLA Modules:
  0.0 222.2 jit_solution(3712524529256751991)
XLA Ops:
  0.6 32.0 %shard_map.246 = (bf16[2,512,512]{2,1,0:T(8,128)(2,1)}, bf16[25,512,512]{2,1,0:T(8,128)(2,1)}, bf16[3,416,2048]{2,1,0:T(8,128)(2,1)}, f32[3,416,2048]{2,1,0:T(8,...) custom-call(f32[4,128,512]{2,1,0:T(8,128)} %refs_1_.3, ...), custom_call_target="tpu_custom_call" | custom-call | flops 30000001024 | bytes 50000000 | tf_op jit(solution)/shard_map/pallas_call | solution.py:500
  32.7 141.4 %shard_map.247 = (bf16[29,512,512]{2,1,0:T(8,128)(2,1)}, f32[29,4,512]{2,1,0:T(4,128)}, f32[29,4,512]{2,1,0:T(4,128)}) custom-call(bf16[2,512,512]{2,1,0:T(8,128)(2,1)} %get-tuple-element.37.refs_0_, bf16[25,512,512]{2,1,0:T(8,128)(2,1)} %get-tuple-element.38.refs_1_, bf16[3,416,2048]{2,1,0:T(8,128)(2,1)} %get-tuple-element.39.refs_2_, ...), custom_call_target="tpu_custom_call" | custom-call | flops 10000000000 | bytes 60000000 | tf_op jit(solution)/shard_map/pallas_call | solution.py:705
  174.2 47.9 %shard_map.248 = (f32[2,1000]{1,0:T(2,128)}, f32[4,128,512]{2,1,0:T(8,128)}, f32[4,512,128]{2,1,0:T(8,128)}, f32[512,512]{1,0:T(8,128)}, f32[3,512,2048]{2,1,0:T...) custom-call(bf16[29,512,512]{2,1,0:T(8,128)(2,1)} %get-tuple-element, ...), custom_call_target="tpu_custom_call" | custom-call | flops 10000000000 | bytes 135000000 | tf_op jit(solution)/shard_map/pallas_call | solution.py:878
